TPU v7x, 256 devices: a whole 4x4x8 slice. The times are simulated.
256 devices in a mesh: gx: 16 (over z, core), gy: 4 (over y), ma: 4 (over x).
Axes of the slice: x: 4, y: 4, z: 8, core: 2. Of those that a mesh axis runs over, the one named last changes fastest.
Arguments:
- object_field: float32 [2, 2048, 1024], P(None, 'gx', 'gy'), may hold values from -5 to 5
- probe_modes: float32 [8, 2, 256, 256], P('ma'), may hold values from -1.5 to 1.5
- measured: float32 [16, 4, 2, 256, 256], P('gx', 'gy'), may hold values from 0.1 to 4
- positions: int32 [16, 4, 2, 2], P('gx', 'gy'), may hold values from 0 to 255, as said below
- slot_counts: int32 [16, 4], P('gx', 'gy'), may hold values from 1 to 2, as said below
Outputs:
- updated_object: float32 [2, 2048, 1024], P(None, 'gx', 'gy')
Inputs may be any that keep to these rules, and one draw needn't show every extreme that they name: positions[a, b, s] holds a row 0 to 127 and a column 0 to 255 of tile (a, b); slots s >= slot_counts[a, b] are unused. `slot_counts`: some tile uses all 2 slots.
All inputs are finite; a program needn't handle non-finite values.
Results may differ from a plain program's by a relative error of at most 0.0023.
Values sent between devices are 32-bit elements; how exact they have to be, the bound alone decides.
A program may use at most 64 MiB of HBM per device.

v0:
```python
import math

import jax
import jax.numpy as jnp
from jax import lax
from jax.sharding import Mesh
from jax.sharding import PartitionSpec as P

OUTER = 2
GX = ("gx_0", "gx_1")
GX_GY_MA = ("gx_0", "gx_1", "gy", "ma")


DAMPING = 1.0


def padded_2(block, sides, width):
    for axis, dim in sides:
        count = lax.axis_size(axis)
        forward = [(i, i + 1) for i in range(count - 1)]
        backward = [(target, source) for source, target in forward]
        low = lax.ppermute(
            lax.slice_in_dim(block, block.shape[dim] - width, None, axis=dim), axis, forward
        )
        high = lax.ppermute(lax.slice_in_dim(block, 0, width, axis=dim), axis, backward)
        block = jnp.concatenate([low, block, high], axis=dim)
    return block


def from_everyone(value, axis):
    copies = jnp.broadcast_to(value, (lax.axis_size(axis), *value.shape))
    return lax.all_to_all(copies, axis, split_axis=0, concat_axis=0, tiled=True)


def taken_together(value, axis):
    return from_everyone(value, axis).sum(axis=0)


def cut_along(value, dim, count):
    before, after = (value.shape[:dim], value.shape[dim + 1 :])
    return jnp.moveaxis(value.reshape(*before, count, -1, *after), dim, 0)


def summed_on_arrival(value, axis, dim):
    count = lax.axis_size(axis)
    blocks = lax.all_to_all(cut_along(value, dim, count), axis, 0, 0, tiled=True)
    return jnp.sum(blocks, axis=0)


def joined_along(blocks, dim):
    lengths = list(blocks.shape[1:])
    lengths[dim] *= blocks.shape[0]
    return jnp.moveaxis(blocks, 0, dim).reshape(lengths)


def gather_directly(value, axis, dim):
    return joined_along(from_everyone(value, axis), dim)


def by_axis(value, axes):
    for axis in axes:
        value = lax.psum(value, axis)
    return value


def dft_tables(patch_width):
    ladder = jnp.arange(patch_width, dtype=jnp.int32)
    phases = ladder[:, None] * ladder[None, :] % patch_width
    angles = phases.astype(jnp.float32) * (2.0 * math.pi / patch_width)
    factor = 1.0 / math.sqrt(patch_width)
    real_part = jnp.cos(angles) * factor
    imag_part = -jnp.sin(angles) * factor
    table_one = jnp.concatenate(
        [jnp.concatenate([real_part, -imag_part], 1), jnp.concatenate([imag_part, real_part], 1)], 0
    ).astype(jnp.bfloat16)
    table_two = jnp.concatenate(
        [jnp.concatenate([real_part, imag_part], 1), jnp.concatenate([-imag_part, real_part], 1)], 0
    ).astype(jnp.bfloat16)
    return (table_one, table_two)


def forward_transform(wavefield, tables):
    patch_width = wavefield.shape[-1]
    halfway = jnp.einsum(
        "pqci,bcik->bpqk",
        tables[0].reshape(2, patch_width, 2, patch_width),
        wavefield,
        preferred_element_type=jnp.float32,
    ).astype(jnp.bfloat16)
    return jnp.einsum(
        "bcik,ckl->bil",
        halfway,
        tables[1].reshape(2, patch_width, 2 * patch_width),
        preferred_element_type=jnp.float32,
    )


def adjoint_transform(weighted, tables):
    patch_width = weighted.shape[1]
    halfway = jnp.einsum(
        "bik,kl->bil", weighted, tables[0], preferred_element_type=jnp.float32
    ).astype(jnp.bfloat16)
    return jnp.einsum(
        "pqci,bicl->bpql",
        tables[1].reshape(2, patch_width, 2, patch_width),
        halfway.reshape(halfway.shape[0], patch_width, 2, patch_width),
        preferred_element_type=jnp.float32,
    )


def exit_waves(probe_modes, windows):
    probe_real = probe_modes[None, :, 0]
    probe_imag = probe_modes[None, :, 1]
    window_real = windows[:, None, 0]
    window_imag = windows[:, None, 1]
    real_part = probe_real * window_real - probe_imag * window_imag
    imag_part = probe_real * window_imag + probe_imag * window_real
    wavefield = jnp.stack([real_part, imag_part], 2).astype(jnp.bfloat16)
    return wavefield.reshape(-1, 2, probe_modes.shape[-1], probe_modes.shape[-1])


def intensity_part(spectra, mode_count):
    patch_width = spectra.shape[1]
    grouped = spectra.reshape(-1, mode_count, patch_width, 2 * patch_width)
    squared = grouped * grouped
    return jnp.sum(squared[..., :patch_width] + squared[..., patch_width:], axis=1)


def change_part(spectra, moved_spectra, mode_count):
    patch_width = spectra.shape[1]
    grouped = spectra.reshape(-1, mode_count, patch_width, 2 * patch_width)
    shifted = moved_spectra.reshape(-1, mode_count, patch_width, 2 * patch_width)
    product = grouped * shifted
    return 2.0 * jnp.sum(product[..., :patch_width] + product[..., patch_width:], axis=1)


def mode_images(weights, spectra, probe_modes, tables):
    mode_count = probe_modes.shape[0]
    patch_width = probe_modes.shape[-1]
    doubled = jnp.concatenate([weights, weights], -1)
    grouped = spectra.reshape(-1, mode_count, patch_width, 2 * patch_width)
    weighted = (2.0 * grouped * doubled[:, None]).astype(jnp.bfloat16)
    returned = adjoint_transform(weighted.reshape(-1, patch_width, 2 * patch_width), tables)
    returned = returned.reshape(-1, mode_count, 2, patch_width, patch_width)
    probe_real = probe_modes[None, :, 0]
    probe_imag = probe_modes[None, :, 1]
    real_part = jnp.sum(probe_real * returned[:, :, 0] + probe_imag * returned[:, :, 1], axis=1)
    imag_part = jnp.sum(probe_real * returned[:, :, 1] - probe_imag * returned[:, :, 0], axis=1)
    return jnp.stack([real_part, imag_part], 1)


def fold_edges(widened, axis_dim, length, rim_width):
    middle = lax.slice_in_dim(widened, 2 * rim_width, 2 * rim_width + length, axis=axis_dim)
    low_rim = lax.slice_in_dim(widened, 0, rim_width, axis=axis_dim)
    high_rim = lax.slice_in_dim(
        widened, length + 3 * rim_width, length + 4 * rim_width, axis=axis_dim
    )
    low_pads = [(0, 0), (0, 0), (0, 0)]
    high_pads = [(0, 0), (0, 0), (0, 0)]
    low_pads[axis_dim] = (0, length - rim_width)
    high_pads[axis_dim] = (length - rim_width, 0)
    return middle + jnp.pad(low_rim, low_pads) + jnp.pad(high_rim, high_pads)


def shards(object_field, probe_modes, measured, positions, slot_counts):
    patch_width = probe_modes.shape[-1]
    mode_count = probe_modes.shape[0]
    rim_width = patch_width // 2
    tile_rows = object_field.shape[1]
    tile_cols = object_field.shape[2]
    slot_count = measured.shape[2]
    tables = dft_tables(patch_width)
    targets = measured[0, 0]
    centres = positions[0, 0]
    live_mask = (jnp.arange(slot_count, dtype=jnp.int32) < slot_counts[0, 0]).astype(jnp.float32)[
        :, None, None
    ]
    anchor = jnp.zeros((), jnp.int32)

    def spectra_of(current):
        padded = padded_2(current, ((GX, 1), ("gy", 2)), rim_width)
        windows = jnp.stack(
            [
                lax.dynamic_slice(
                    padded,
                    (anchor, centres[slot_index, 0], centres[slot_index, 1]),
                    (2, patch_width, patch_width),
                )
                for slot_index in range(slot_count)
            ],
            0,
        )
        return forward_transform(exit_waves(probe_modes, windows), tables)

    def mode_total(partial_value):
        return taken_together(partial_value, "ma")

    def combine(folded):
        summed = summed_on_arrival(folded, "ma", 1)
        return summed

    def project(weights, spectra):
        pieces = mode_images(weights, spectra, probe_modes, tables)
        extended = jnp.zeros((2, tile_rows + patch_width, tile_cols + patch_width), jnp.float32)
        for slot_index in range(slot_count):
            corner = (anchor, centres[slot_index, 0], centres[slot_index, 1])
            extended = lax.dynamic_update_slice(
                extended,
                lax.dynamic_slice(extended, corner, (2, patch_width, patch_width))
                + pieces[slot_index],
                corner,
            )
        widened = padded_2(extended, ((GX, 1), ("gy", 2)), rim_width)
        folded = fold_edges(fold_edges(widened, 1, tile_rows, rim_width), 2, tile_cols, rim_width)
        result = combine(folded)
        return result

    def to_whole(vector):
        whole = gather_directly(vector, "ma", 1)
        return whole

    def local_sum(first_vec, second_vec):
        return jnp.sum(first_vec * second_vec)

    current = object_field
    for outer_step in range(OUTER):
        spectra = spectra_of(current)
        misfit = live_mask * (mode_total(intensity_part(spectra, mode_count)) - targets)
        gradient = project(misfit, spectra)
        residual = -gradient
        direction = residual
        norm_now = by_axis(local_sum(residual, residual), GX_GY_MA)
        moved_spectra = spectra_of(to_whole(direction))
        change = live_mask * mode_total(change_part(spectra, moved_spectra, mode_count))
        applied = project(change, spectra) + DAMPING * direction
        step_size = norm_now / by_axis(local_sum(direction, applied), GX_GY_MA)
        update = step_size * direction
        residual = residual - step_size * applied
        current = current + to_whole(update)
    return current


def solution(mesh):
    finer = Mesh(
        mesh.devices.reshape(8, 2, mesh.shape["gy"], mesh.shape["ma"]), ("gx_0", "gx_1", "gy", "ma")
    )
    placed = (
        P(None, GX, "gy"),
        P("ma", None, None, None),
        P(GX, "gy", None, None, None),
        P(GX, "gy", None, None),
        P(GX, "gy"),
    )
    return jax.shard_map(
        shards, mesh=finer, in_specs=placed, out_specs=P(None, GX, "gy"), check_vma=False
    )
```

profile of v0, /device:TPU:8, one launch (start us, length us, event | category | flops | bytes accessed | tf_op | source)
XLA Modules:
  0.0 656.8 jit_solution(18152097577675178432)
XLA Ops:
  39.3 21.9 %all-to-all-done = f32[4,2,256,256]{3,2,1,0:T(8,128)} async-done(((f32[4,2,256,256]{3,2,1,0:T(8,128)}), f32[4,2,256,256]{3,2,1,0:T(8,128)}, u32[]{:S(2)}, u32[]{:S(2)}) %all-to-all-start) | async-done | bytes 2097184 | tf_op jit(solution)/shard_map/all_to_all | solution.py:32
  119.9 9.1 %all_to_all.64 = f32[4,2,32,256]{3,2,1,0:T(8,128)S(1)} all-to-all(f32[4,2,32,256]{3,2,1,0:T(8,128)S(1)} %copy.194), channel_id=1, replica_groups=mesh['gx_0'=8,'gx_1'=2,'gy'=4,'ma'=4] {'ma'}, dimensions={0} | all-to-all | bytes 524288 | tf_op jit(solution)/shard_map/all_to_all | solution.py:46
  129.1 9.1 %all_to_all.60 = f32[4,2,32,256]{3,2,1,0:T(8,128)S(1)} all-to-all(f32[4,2,32,256]{3,2,1,0:T(8,128)S(1)} %broadcast_in_dim.32), channel_id=1, replica_groups=mesh['gx_0'=8,'gx_1'=2,'gy'=4,'ma'=4] {'ma'}, dimensions={0} | all-to-all | bytes 524288 | tf_op jit(solution)/shard_map/all_to_all | solution.py:32
  145.4 11.8 %collective-permute-done.9 = f32[2,128,256]{2,1,0:T(8,128)S(1)} collective-permute-done((f32[2,128,256]{2,1,0:T(8,128)S(1)}, f32[2,128,256]{2,1,0:T(8,128)S(1)}, u32[]{:S(2)}, u32[]{:S(2)}) %collective-permute-start.9) | collective-permute-done | bytes 262176 | tf_op jit(solution)/shard_map/ppermute | solution.py:25
  175.7 28.6 %all_to_all.65 = f32[4,2,256,256]{3,2,1,0:T(8,128)} all-to-all(f32[4,2,256,256]{3,2,1,0:T(8,128)S(1)} %broadcast_in_dim.33), channel_id=1, replica_groups=mesh['gx_0'=8,'gx_1'=2,'gy'=4,'ma'=4] {'ma'}, dimensions={0} | all-to-all | bytes 4194304 | tf_op jit(solution)/shard_map/all_to_all | solution.py:32
  238.0 8.4 %collective-permute-done.13 = f32[2,128,512]{1,2,0:T(8,128)S(1)} collective-permute-done((f32[2,128,512]{1,2,0:T(8,128)S(1)}, f32[2,128,512]{1,2,0:T(8,128)S(1)}, u32[]{:S(2)}, u32[]{:S(2)}) %collective-permute-start.13) | collective-permute-done | bytes 524320 | tf_op jit(solution)/shard_map/ppermute | solution.py:25
  261.8 9.1 %all_to_all.66 = f32[4,2,32,256]{3,2,1,0:T(8,128)S(1)} all-to-all(f32[4,2,32,256]{3,2,1,0:T(8,128)S(1)} %copy.205), channel_id=1, replica_groups=mesh['gx_0'=8,'gx_1'=2,'gy'=4,'ma'=4] {'ma'}, dimensions={0} | all-to-all | bytes 524288 | tf_op jit(solution)/shard_map/all_to_all | solution.py:46
  271.5 27.1 %all-reduce.5 = (f32[]{:T(128)}, f32[]{:T(128)}) all-reduce(f32[]{:T(128)} %get-tuple-element.16, f32[]{:T(128)} %get-tuple-element.15), channel_id=1, replica_groups=mesh['gx_0'=8,'gx_1'=2,'gy'=4,'ma'=4] {'gx_0'}, use_global_device_ids=true, to_apply=%region_6.7 | all-reduce | flops 2 | bytes 16 | tf_op jit(solution)/shard_map/psum | solution.py:62
  301.8 9.6 %all-reduce.9 = (f32[]{:T(128)}, f32[]{:T(128)}) all-reduce(f32[]{:T(128)} %get-tuple-element.31, f32[]{:T(128)} %get-tuple-element.32), channel_id=1, replica_groups=mesh['gx_0'=8,'gx_1'=2,'gy'=4,'ma'=4] {'gy'}, use_global_device_ids=true, to_apply=%region_8.9 | all-reduce | flops 2 | bytes 16 | tf_op jit(solution)/shard_map/psum | solution.py:62
  311.4 9.5 %all-reduce.7 = (f32[]{:T(128)}, f32[]{:T(128)}) all-reduce(f32[]{:T(128)} %get-tuple-element.27, f32[]{:T(128)} %get-tuple-element.28), channel_id=1, replica_groups=mesh['gx_0'=8,'gx_1'=2,'gy'=4,'ma'=4] {'ma'}, use_global_device_ids=true, to_apply=%region_9.10 | all-reduce | flops 2 | bytes 16 | tf_op jit(solution)/shard_map/psum | solution.py:62
  322.3 9.1 %all_to_all.61 = f32[4,2,32,256]{3,2,1,0:T(8,128)S(1)} all-to-all(f32[4,2,32,256]{3,2,1,0:T(8,128)S(1)} %broadcast_in_dim.34), channel_id=1, replica_groups=mesh['gx_0'=8,'gx_1'=2,'gy'=4,'ma'=4] {'ma'}, dimensions={0} | all-to-all | bytes 524288 | tf_op jit(solution)/shard_map/all_to_all | solution.py:32
  354.3 28.5 %all_to_all.67 = f32[4,2,256,256]{3,2,1,0:T(8,128)} all-to-all(f32[4,2,256,256]{3,2,1,0:T(8,128)S(1)} %broadcast_in_dim.35), channel_id=1, replica_groups=mesh['gx_0'=8,'gx_1'=2,'gy'=4,'ma'=4] {'ma'}, dimensions={0} | all-to-all | bytes 4194304 | tf_op jit(solution)/shard_map/all_to_all | solution.py:32
  417.0 10.5 %collective-permute-done.21 = f32[2,128,512]{1,2,0:T(8,128)S(1)} collective-permute-done((f32[2,128,512]{1,2,0:T(8,128)S(1)}, f32[2,128,512]{1,2,0:T(8,128)S(1)}, u32[]{:S(2)}, u32[]{:S(2)}) %collective-permute-start.21) | collective-permute-done | bytes 524320 | tf_op jit(solution)/shard_map/ppermute | solution.py:25
  443.7 9.1 %all_to_all.68 = f32[4,2,32,256]{3,2,1,0:T(8,128)S(1)} all-to-all(f32[4,2,32,256]{3,2,1,0:T(8,128)S(1)} %copy.216), channel_id=1, replica_groups=mesh['gx_0'=8,'gx_1'=2,'gy'=4,'ma'=4] {'ma'}, dimensions={0} | all-to-all | bytes 524288 | tf_op jit(solution)/shard_map/all_to_all | solution.py:46
  452.9 9.1 %all_to_all.62 = f32[4,2,32,256]{3,2,1,0:T(8,128)S(1)} all-to-all(f32[4,2,32,256]{3,2,1,0:T(8,128)S(1)} %broadcast_in_dim.36), channel_id=1, replica_groups=mesh['gx_0'=8,'gx_1'=2,'gy'=4,'ma'=4] {'ma'}, dimensions={0} | all-to-all | bytes 524288 | tf_op jit(solution)/shard_map/all_to_all | solution.py:32
  469.0 9.7 %collective-permute-done.25 = f32[2,128,256]{2,1,0:T(8,128)S(1)} collective-permute-done((f32[2,128,256]{2,1,0:T(8,128)S(1)}, f32[2,128,256]{2,1,0:T(8,128)S(1)}, u32[]{:S(2)}, u32[]{:S(2)}) %collective-permute-start.25) | collective-permute-done | bytes 262176 | tf_op jit(solution)/shard_map/ppermute | solution.py:25
  495.5 28.9 %all_to_all.69 = f32[4,2,256,256]{3,2,1,0:T(8,128)} all-to-all(f32[4,2,256,256]{3,2,1,0:T(8,128)S(1)} %broadcast_in_dim.37), channel_id=1, replica_groups=mesh['gx_0'=8,'gx_1'=2,'gy'=4,'ma'=4] {'ma'}, dimensions={0} | all-to-all | bytes 4194304 | tf_op jit(solution)/shard_map/all_to_all | solution.py:32
  534.4 8.8 %dynamic_update_slice.30 = f32[2,384,512]{1,2,0:T(8,128)S(1)} dynamic-update-slice(f32[2,384,512]{1,2,0:T(8,128)S(1)} %broadcast.214, f32[2,256,256]{1,2,0:T(8,128)S(1)} %fusion.25, s32[]{:T(128)} %constant.27.clone.1, s32[]{:T(128)S(6)} %select_n.29, s32[]{:T(128)S(6)} %select_n.30) | dynamic-update-slice | bytes 1048580 | tf_op jit(solution)/shard_map/dynamic_update_slice | solution.py:207
  557.9 9.6 %collective-permute-done.29 = f32[2,128,512]{1,2,0:T(8,128)S(1)} collective-permute-done((f32[2,128,512]{1,2,0:T(8,128)S(1)}, f32[2,128,512]{1,2,0:T(8,128)S(1)}, u32[]{:S(2)}, u32[]{:S(2)}) %collective-permute-start.29) | collective-permute-done | bytes 524320 | tf_op jit(solution)/shard_map/ppermute | solution.py:25
  583.0 9.1 %all_to_all.70 = f32[4,2,32,256]{3,2,1,0:T(8,128)S(1)} all-to-all(f32[4,2,32,256]{3,2,1,0:T(8,128)S(1)} %copy.227), channel_id=1, replica_groups=mesh['gx_0'=8,'gx_1'=2,'gy'=4,'ma'=4] {'ma'}, dimensions={0} | all-to-all | bytes 524288 | tf_op jit(solution)/shard_map/all_to_all | solution.py:46
  592.7 29.2 %all-reduce.4 = (f32[]{:T(128)}, f32[]{:T(128)}) all-reduce(f32[]{:T(128)} %get-tuple-element.14, f32[]{:T(128)} %get-tuple-element.13), channel_id=1, replica_groups=mesh['gx_0'=8,'gx_1'=2,'gy'=4,'ma'=4] {'gx_0'}, use_global_device_ids=true, to_apply=%region_26.27 | all-reduce | flops 2 | bytes 16 | tf_op jit(solution)/shard_map/psum | solution.py:62
  625.0 10.7 %all-reduce.8 = (f32[]{:T(128)}, f32[]{:T(128)}) all-reduce(f32[]{:T(128)} %get-tuple-element.29, f32[]{:T(128)} %get-tuple-element.30), channel_id=1, replica_groups=mesh['gx_0'=8,'gx_1'=2,'gy'=4,'ma'=4] {'gy'}, use_global_device_ids=true, to_apply=%region_28.29 | all-reduce | flops 2 | bytes 16 | tf_op jit(solution)/shard_map/psum | solution.py:62
  635.7 9.5 %all-reduce.6 = (f32[]{:T(128)}, f32[]{:T(128)}) all-reduce(f32[]{:T(128)} %get-tuple-element.25, f32[]{:T(128)} %get-tuple-element.26), channel_id=1, replica_groups=mesh['gx_0'=8,'gx_1'=2,'gy'=4,'ma'=4] {'ma'}, use_global_device_ids=true, to_apply=%region_29.30 | all-reduce | flops 2 | bytes 16 | tf_op jit(solution)/shard_map/psum | solution.py:62
  646.6 9.1 %all_to_all.63 = f32[4,2,32,256]{3,2,1,0:T(8,128)S(1)} all-to-all(f32[4,2,32,256]{3,2,1,0:T(8,128)S(1)} %broadcast_in_dim.38), channel_id=1, replica_groups=mesh['gx_0'=8,'gx_1'=2,'gy'=4,'ma'=4] {'ma'}, dimensions={0} | all-to-all | bytes 524288 | tf_op jit(solution)/shard_map/all_to_all | solution.py:32
  (281 shorter events, 308.7 us)
Async XLA Ops:
  8.2 18.0 %collective-permute-start.2 = (f32[2,384,128]{2,1,0:T(8,128)}, f32[2,384,128]{2,1,0:T(8,128)S(1)}, u32[]{:S(2)}, u32[]{:S(2)}) collective-permute-start(f32[2,384,128]{2,1,0:T(8,128)} %get-tuple-element.81), channel_id=1, source_target_pairs={{0,4},{4,8},{8,12},{1,5},{5,9},{9,13},{2,6},{6,10},{10,14},{3,7},{... | collective-permute-start | bytes 1179656 | tf_op jit(solution)/shard_map/ppermute | solution.py:22
  11.7 14.6 %collective-permute-start.3 = (f32[2,384,128]{2,1,0:T(8,128)}, f32[2,384,128]{2,1,0:T(8,128)}, u32[]{:S(2)}, u32[]{:S(2)}) collective-permute-start(f32[2,384,128]{2,1,0:T(8,128)} %get-tuple-element.82), channel_id=1, source_target_pairs={{4,0},{8,4},{12,8},{5,1},{9,5},{13,9},{6,2},{10,6},{14,10},{7,3},{... | collective-permute-start | bytes 1179656 | tf_op jit(solution)/shard_map/ppermute | solution.py:25
  32.2 29.0 %all-to-all-start = ((f32[4,2,256,256]{3,2,1,0:T(8,128)}), f32[4,2,256,256]{3,2,1,0:T(8,128)}, u32[]{:S(2)}, u32[]{:S(2)}) async-start(f32[4,2,256,256]{3,2,1,0:T(8,128)} %broadcast_in_dim.31), calls=%async_computation | async-start | bytes 4194304 | tf_op jit(solution)/shard_map/all_to_all | solution.py:32
  94.5 8.8 %collective-permute-start.5 = (f32[2,128,512]{1,2,0:T(8,128)S(1)}, f32[2,128,512]{1,2,0:T(8,128)S(1)}, u32[]{:S(2)}, u32[]{:S(2)}) collective-permute-start(f32[2,128,512]{1,2,0:T(8,128)S(1)} %get-tuple-element.62), channel_id=1, source_target_pairs={{16,0},{32,16},{48,32},{64,48},{80,64},{96,80},{112,96},{128,112},... | collective-permute-start | bytes 1572872 | tf_op jit(solution)/shard_map/ppermute | solution.py:25
  103.4 13.0 %collective-permute-start.6 = (f32[2,640,128]{1,2,0:T(8,128)S(1)}, f32[2,640,128]{1,2,0:T(8,128)S(1)}, u32[]{:S(2)}, u32[]{:S(2)}) collective-permute-start(f32[2,640,128]{1,2,0:T(8,128)S(1)} %get-tuple-element.39), channel_id=1, source_target_pairs={{0,4},{4,8},{8,12},{1,5},{5,9},{9,13},{2,6},{6,10},{10,14},{3,7},{... | collective-permute-start | bytes 1966088 | tf_op jit(solution)/shard_map/ppermute | solution.py:22
  105.9 13.1 %collective-permute-start.7 = (f32[2,640,128]{1,2,0:T(8,128)S(1)}, f32[2,640,128]{1,2,0:T(8,128)S(1)}, u32[]{:S(2)}, u32[]{:S(2)}) collective-permute-start(f32[2,640,128]{1,2,0:T(8,128)S(1)} %get-tuple-element.40), channel_id=1, source_target_pairs={{4,0},{8,4},{12,8},{5,1},{9,5},{13,9},{6,2},{10,6},{14,10},{7,3},{... | collective-permute-start | bytes 1966088 | tf_op jit(solution)/shard_map/ppermute | solution.py:25
  138.1 7.3 %collective-permute-start.8 = (f32[2,128,256]{2,1,0:T(8,128)S(1)}, f32[2,128,256]{2,1,0:T(8,128)S(1)}, u32[]{:S(2)}, u32[]{:S(2)}) collective-permute-start(f32[2,128,256]{2,1,0:T(8,128)S(1)} %bitcast.382), channel_id=1, source_target_pairs={{0,16},{16,32},{32,48},{48,64},{64,80},{80,96},{96,112},{112,128},... | collective-permute-start | bytes 786440 | tf_op jit(solution)/shard_map/ppermute | solution.py:22
  144.1 13.1 %collective-permute-start.9 = (f32[2,128,256]{2,1,0:T(8,128)S(1)}, f32[2,128,256]{2,1,0:T(8,128)S(1)}, u32[]{:S(2)}, u32[]{:S(2)}) collective-permute-start(f32[2,128,256]{2,1,0:T(8,128)S(1)} %bitcast.383), channel_id=1, source_target_pairs={{16,0},{32,16},{48,32},{64,48},{80,64},{96,80},{112,96},{128,112},... | collective-permute-start | bytes 786440 | tf_op jit(solution)/shard_map/ppermute | solution.py:25
  157.3 10.1 %collective-permute-start.10 = (f32[2,384,128]{2,1,0:T(8,128)S(1)}, f32[2,384,128]{2,1,0:T(8,128)S(1)}, u32[]{:S(2)}, u32[]{:S(2)}) collective-permute-start(f32[2,384,128]{2,1,0:T(8,128)S(1)} %get-tuple-element.79), channel_id=1, source_target_pairs={{0,4},{4,8},{8,12},{1,5},{5,9},{9,13},{2,6},{6,10},{10,14},{3,7},{... | collective-permute-start | bytes 1179656 | tf_op jit(solution)/shard_map/ppermute | solution.py:22
  161.2 10.4 %collective-permute-start.11 = (f32[2,384,128]{2,1,0:T(8,128)S(1)}, f32[2,384,128]{2,1,0:T(8,128)S(1)}, u32[]{:S(2)}, u32[]{:S(2)}) collective-permute-start(f32[2,384,128]{2,1,0:T(8,128)S(1)} %get-tuple-element.80), channel_id=1, source_target_pairs={{4,0},{8,4},{12,8},{5,1},{9,5},{13,9},{6,2},{10,6},{14,10},{7,3},{... | collective-permute-start | bytes 1179656 | tf_op jit(solution)/shard_map/ppermute | solution.py:25
  236.5 9.9 %collective-permute-start.13 = (f32[2,128,512]{1,2,0:T(8,128)S(1)}, f32[2,128,512]{1,2,0:T(8,128)S(1)}, u32[]{:S(2)}, u32[]{:S(2)}) collective-permute-start(f32[2,128,512]{1,2,0:T(8,128)S(1)} %get-tuple-element.58), channel_id=1, source_target_pairs={{16,0},{32,16},{48,32},{64,48},{80,64},{96,80},{112,96},{128,112},... | collective-permute-start | bytes 1572872 | tf_op jit(solution)/shard_map/ppermute | solution.py:25
  246.5 13.0 %collective-permute-start.14 = (f32[2,640,128]{1,2,0:T(8,128)S(1)}, f32[2,640,128]{1,2,0:T(8,128)S(1)}, u32[]{:S(2)}, u32[]{:S(2)}) collective-permute-start(f32[2,640,128]{1,2,0:T(8,128)S(1)} %get-tuple-element.37), channel_id=1, source_target_pairs={{0,4},{4,8},{8,12},{1,5},{5,9},{9,13},{2,6},{6,10},{10,14},{3,7},{... | collective-permute-start | bytes 1966088 | tf_op jit(solution)/shard_map/ppermute | solution.py:22
  248.4 13.0 %collective-permute-start.15 = (f32[2,640,128]{1,2,0:T(8,128)S(1)}, f32[2,640,128]{1,2,0:T(8,128)S(1)}, u32[]{:S(2)}, u32[]{:S(2)}) collective-permute-start(f32[2,640,128]{1,2,0:T(8,128)S(1)} %get-tuple-element.38), channel_id=1, source_target_pairs={{4,0},{8,4},{12,8},{5,1},{9,5},{13,9},{6,2},{10,6},{14,10},{7,3},{... | collective-permute-start | bytes 1966088 | tf_op jit(solution)/shard_map/ppermute | solution.py:25
  338.5 10.1 %collective-permute-start.18 = (f32[2,384,128]{2,1,0:T(8,128)S(1)}, f32[2,384,128]{2,1,0:T(8,128)S(1)}, u32[]{:S(2)}, u32[]{:S(2)}) collective-permute-start(f32[2,384,128]{2,1,0:T(8,128)S(1)} %get-tuple-element.77), channel_id=1, source_target_pairs={{0,4},{4,8},{8,12},{1,5},{5,9},{9,13},{2,6},{6,10},{10,14},{3,7},{... | collective-permute-start | bytes 1179656 | tf_op jit(solution)/shard_map/ppermute | solution.py:22
  340.5 10.1 %collective-permute-start.19 = (f32[2,384,128]{2,1,0:T(8,128)S(1)}, f32[2,384,128]{2,1,0:T(8,128)S(1)}, u32[]{:S(2)}, u32[]{:S(2)}) collective-permute-start(f32[2,384,128]{2,1,0:T(8,128)S(1)} %get-tuple-element.78), channel_id=1, source_target_pairs={{4,0},{8,4},{12,8},{5,1},{9,5},{13,9},{6,2},{10,6},{14,10},{7,3},{... | collective-permute-start | bytes 1179656 | tf_op jit(solution)/shard_map/ppermute | solution.py:25
  415.5 12.0 %collective-permute-start.21 = (f32[2,128,512]{1,2,0:T(8,128)S(1)}, f32[2,128,512]{1,2,0:T(8,128)S(1)}, u32[]{:S(2)}, u32[]{:S(2)}) collective-permute-start(f32[2,128,512]{1,2,0:T(8,128)S(1)} %get-tuple-element.54), channel_id=1, source_target_pairs={{16,0},{32,16},{48,32},{64,48},{80,64},{96,80},{112,96},{128,112},... | collective-permute-start | bytes 1572872 | tf_op jit(solution)/shard_map/ppermute | solution.py:25
  427.6 13.0 %collective-permute-start.22 = (f32[2,640,128]{1,2,0:T(8,128)S(1)}, f32[2,640,128]{1,2,0:T(8,128)S(1)}, u32[]{:S(2)}, u32[]{:S(2)}) collective-permute-start(f32[2,640,128]{1,2,0:T(8,128)S(1)} %get-tuple-element.35), channel_id=1, source_target_pairs={{0,4},{4,8},{8,12},{1,5},{5,9},{9,13},{2,6},{6,10},{10,14},{3,7},{... | collective-permute-start | bytes 1966088 | tf_op jit(solution)/shard_map/ppermute | solution.py:22
  430.1 13.3 %collective-permute-start.23 = (f32[2,640,128]{1,2,0:T(8,128)S(1)}, f32[2,640,128]{1,2,0:T(8,128)S(1)}, u32[]{:S(2)}, u32[]{:S(2)}) collective-permute-start(f32[2,640,128]{1,2,0:T(8,128)S(1)} %get-tuple-element.36), channel_id=1, source_target_pairs={{4,0},{8,4},{12,8},{5,1},{9,5},{13,9},{6,2},{10,6},{14,10},{7,3},{... | collective-permute-start | bytes 1966088 | tf_op jit(solution)/shard_map/ppermute | solution.py:25
  467.6 11.0 %collective-permute-start.25 = (f32[2,128,256]{2,1,0:T(8,128)S(1)}, f32[2,128,256]{2,1,0:T(8,128)S(1)}, u32[]{:S(2)}, u32[]{:S(2)}) collective-permute-start(f32[2,128,256]{2,1,0:T(8,128)S(1)} %bitcast.387), channel_id=1, source_target_pairs={{16,0},{32,16},{48,32},{64,48},{80,64},{96,80},{112,96},{128,112},... | collective-permute-start | bytes 786440 | tf_op jit(solution)/shard_map/ppermute | solution.py:25
  478.7 10.1 %collective-permute-start.26 = (f32[2,384,128]{2,1,0:T(8,128)S(1)}, f32[2,384,128]{2,1,0:T(8,128)S(1)}, u32[]{:S(2)}, u32[]{:S(2)}) collective-permute-start(f32[2,384,128]{2,1,0:T(8,128)S(1)} %get-tuple-element.75), channel_id=1, source_target_pairs={{0,4},{4,8},{8,12},{1,5},{5,9},{9,13},{2,6},{6,10},{10,14},{3,7},{... | collective-permute-start | bytes 1179656 | tf_op jit(solution)/shard_map/ppermute | solution.py:22
  481.0 10.4 %collective-permute-start.27 = (f32[2,384,128]{2,1,0:T(8,128)S(1)}, f32[2,384,128]{2,1,0:T(8,128)S(1)}, u32[]{:S(2)}, u32[]{:S(2)}) collective-permute-start(f32[2,384,128]{2,1,0:T(8,128)S(1)} %get-tuple-element.76), channel_id=1, source_target_pairs={{4,0},{8,4},{12,8},{5,1},{9,5},{13,9},{6,2},{10,6},{14,10},{7,3},{... | collective-permute-start | bytes 1179656 | tf_op jit(solution)/shard_map/ppermute | solution.py:25
  556.4 11.1 %collective-permute-start.29 = (f32[2,128,512]{1,2,0:T(8,128)S(1)}, f32[2,128,512]{1,2,0:T(8,128)S(1)}, u32[]{:S(2)}, u32[]{:S(2)}) collective-permute-start(f32[2,128,512]{1,2,0:T(8,128)S(1)} %get-tuple-element.50), channel_id=1, source_target_pairs={{16,0},{32,16},{48,32},{64,48},{80,64},{96,80},{112,96},{128,112},... | collective-permute-start | bytes 1572872 | tf_op jit(solution)/shard_map/ppermute | solution.py:25
  567.6 13.0 %collective-permute-start.30 = (f32[2,640,128]{1,2,0:T(8,128)S(1)}, f32[2,640,128]{1,2,0:T(8,128)S(1)}, u32[]{:S(2)}, u32[]{:S(2)}) collective-permute-start(f32[2,640,128]{1,2,0:T(8,128)S(1)} %get-tuple-element.33), channel_id=1, source_target_pairs={{0,4},{4,8},{8,12},{1,5},{5,9},{9,13},{2,6},{6,10},{10,14},{3,7},{... | collective-permute-start | bytes 1966088 | tf_op jit(solution)/shard_map/ppermute | solution.py:22
  569.6 13.0 %collective-permute-start.31 = (f32[2,640,128]{1,2,0:T(8,128)S(1)}, f32[2,640,128]{1,2,0:T(8,128)S(1)}, u32[]{:S(2)}, u32[]{:S(2)}) collective-permute-start(f32[2,640,128]{1,2,0:T(8,128)S(1)} %get-tuple-element.34), channel_id=1, source_target_pairs={{4,0},{8,4},{12,8},{5,1},{9,5},{13,9},{6,2},{10,6},{14,10},{7,3},{... | collective-permute-start | bytes 1966088 | tf_op jit(solution)/shard_map/ppermute | solution.py:25
  (38 other events, 242.7 us)
where the time goes:
time: 666 us; the launch traced here: 657 us
  blocking collectives  260 us (39%)
  waiting for transfers between devices  146 us (22%)
  starting transfers between devices  94.3 us (14%)
  local copies, waits for them, and re-layouts  88.7 us (13%)
  other arithmetic  38.9 us (6%)
  matrix products  15.6 us (2%)
  between operations  13.3 us (2%)
    all_to_all x7, blocking collectives, from_everyone(): return lax.all_to_all(copies, axis, split_axis=0, concat_axis=0, tiled=True)  122 us
    psum x8, blocking collectives, by_axis(): value = lax.psum(value, axis)  102 us
    ppermute x16, waiting for transfers between devices, padded_2(): lax.ppermute(lax.slice_in_dim(block, 0, width, axis=dim), axis, backward)  82 us
    dynamic_update_slice x8, local copies, waits for them, and re-layouts, project(): lax.dynamic_update_slice(extended, lax.dynamic_slice(extended, corner, (2...  64 us
    ppermute x16, starting transfers between devices, padded_2(): lax.ppermute(lax.slice_in_dim(block, block.shape[dim] - width, None, axis...  52.6 us
    ppermute x16, waiting for transfers between devices, padded_2(): lax.ppermute(lax.slice_in_dim(block, block.shape[dim] - width, None, axis...  41.6 us
    ppermute x16, starting transfers between devices, padded_2(): lax.ppermute(lax.slice_in_dim(block, 0, width, axis=dim), axis, backward)  37.2 us
    all_to_all x4, blocking collectives, summed_on_arrival(): lax.all_to_all(cut_along(value, dim, count), axis, 0, 0, tiled=True)  36.3 us
  transfers between devices with their start and end apart: 33, of which 27 were waited for; matrix products, arithmetic and copies ran while one was open for 1% of the time, Pallas kernels for 0%

commit v1 on v0

--- a/solution.py
+++ b/solution.py
@@ -8,7 +8,7 @@
 
 OUTER = 2
 GX = ("gx_0", "gx_1")
-GX_GY_MA = ("gx_0", "gx_1", "gy", "ma")
+GX_GY = ("gx_0", "gx_1", "gy")
 
 
 DAMPING = 1.0
@@ -55,12 +55,6 @@
 
 def gather_directly(value, axis, dim):
     return joined_along(from_everyone(value, axis), dim)
-
-
-def by_axis(value, axes):
-    for axis in axes:
-        value = lax.psum(value, axis)
-    return value
 
 
 def dft_tables(patch_width):
@@ -219,24 +213,23 @@
         whole = gather_directly(vector, "ma", 1)
         return whole
 
-    def local_sum(first_vec, second_vec):
-        return jnp.sum(first_vec * second_vec)
-
     current = object_field
+    spectra = spectra_of(current)
+    intensity = mode_total(intensity_part(spectra, mode_count))
     for outer_step in range(OUTER):
-        spectra = spectra_of(current)
-        misfit = live_mask * (mode_total(intensity_part(spectra, mode_count)) - targets)
-        gradient = project(misfit, spectra)
-        residual = -gradient
-        direction = residual
-        norm_now = by_axis(local_sum(residual, residual), GX_GY_MA)
-        moved_spectra = spectra_of(to_whole(direction))
-        change = live_mask * mode_total(change_part(spectra, moved_spectra, mode_count))
-        applied = project(change, spectra) + DAMPING * direction
-        step_size = norm_now / by_axis(local_sum(direction, applied), GX_GY_MA)
-        update = step_size * direction
-        residual = residual - step_size * applied
-        current = current + to_whole(update)
+        misfit = live_mask * (intensity - targets)
+        direction = to_whole(-project(misfit, spectra))
+        moved_spectra = spectra_of(direction)
+        raw_change = mode_total(change_part(spectra, moved_spectra, mode_count))
+        change = live_mask * raw_change
+        norm_now = jnp.sum(direction * direction)
+        totals = lax.psum(jnp.stack([norm_now, jnp.sum(change * change)]), GX_GY)
+        step_size = totals[0] / (totals[1] + DAMPING * totals[0])
+        current = current + step_size * direction
+        if outer_step + 1 < OUTER:
+            moved_intensity = mode_total(intensity_part(moved_spectra, mode_count))
+            intensity = intensity + step_size * (raw_change + step_size * moved_intensity)
+            spectra = spectra + step_size * moved_spectra
     return current
 
 

time: 666 us -> 641 us (0.962)
  the two profiles are of different devices: /device:TPU:8 before, /device:TPU:128 now
where the time goes in v1:
time: 641 us
  blocking collectives  297 us (46%)
  waiting for transfers between devices  139 us (22%)
  starting transfers between devices  75.1 us (12%)
  local copies, waits for them, and re-layouts  55.7 us (9%)
  other arithmetic  45 us (7%)
  matrix products  16.2 us (3%)
  between operations  12.8 us (2%)
    psum x2, blocking collectives, shards(): totals = lax.psum(jnp.stack([norm_now, jnp.sum(change * change)]), GX_GY)  257 us
    all_to_all x4, waiting for transfers between devices, from_everyone(): return lax.all_to_all(copies, axis, split_axis=0, concat_axis=0, tiled=True)  66.9 us
    ppermute x10, waiting for transfers between devices, padded_2(): lax.ppermute(lax.slice_in_dim(block, block.shape[dim] - width, None, axis...  46.6 us
    ppermute x10, starting transfers between devices, padded_2(): lax.ppermute(lax.slice_in_dim(block, 0, width, axis=dim), axis, backward)  31.1 us
    dynamic_update_slice x4, local copies, waits for them, and re-layouts, project(): lax.dynamic_update_slice(extended, lax.dynamic_slice(extended, corner, (2...  29.9 us
    ppermute x10, starting transfers between devices, padded_2(): lax.ppermute(lax.slice_in_dim(block, block.shape[dim] - width, None, axis...  26.9 us
    ppermute x10, waiting for transfers between devices, padded_2(): lax.ppermute(lax.slice_in_dim(block, 0, width, axis=dim), axis, backward)  25.9 us
    all_to_all x2, blocking collectives, summed_on_arrival(): lax.all_to_all(cut_along(value, dim, count), axis, 0, 0, tiled=True)  21.1 us
  transfers between devices with their start and end apart: 24, of which 21 were waited for; matrix products, arithmetic and copies ran while one was open for 3% of the time, Pallas kernels for 0%

profile of v1, /device:TPU:128, one launch (start us, length us, event | category | flops | bytes accessed | tf_op | source)
XLA Modules:
  0.0 641.0 jit_solution(5719750726592840737)
XLA Ops:
  2.1 4.9 collective-permute-start.1
  47.0 23.9 %all-to-all-done = f32[4,2,256,256]{3,2,1,0:T(8,128)} async-done(((f32[4,2,256,256]{3,2,1,0:T(8,128)}), f32[4,2,256,256]{3,2,1,0:T(8,128)}, u32[]{:S(2)}, u32[]{:S(2)}) %all-to-all-start) | async-done | bytes 2097184 | tf_op jit(solution)/shard_map/all_to_all | solution.py:32
  81.3 7.9 %dynamic_update_slice.12 = f32[2,384,512]{1,2,0:T(8,128)S(1)} dynamic-update-slice(f32[2,384,512]{1,2,0:T(8,128)S(1)} %broadcast.160.clone, f32[2,256,256]{1,2,0:T(8,128)} %fusion.34, s32[]{:T(128)} %constant.12.clone.1, s32[]{:T(128)S(6)} %select_n.53, s32[]{:T(128)S(6)} %select_n.54) | dynamic-update-slice | bytes 1048580 | tf_op jit(solution)/shard_map/dynamic_update_slice | solution.py:201
  91.1 7.1 %dynamic_update_slice.13 = f32[2,384,512]{1,2,0:T(8,128)S(1)} dynamic-update-slice(f32[2,384,512]{1,2,0:T(8,128)S(1)} %dynamic_update_slice.12, f32[2,256,256]{1,2,0:T(8,128)} %fusion.42, s32[]{:T(128)} %constant.12.clone.1, s32[]{:T(128)S(6)} %select_n.55, s32[]{:T(128)S(6)} %select_n.56) | dynamic-update-slice | bytes 1048580 | tf_op jit(solution)/shard_map/dynamic_update_slice | solution.py:201
  100.2 4.9 collective-permute-start.5
  105.1 4.9 collective-permute-done.4
  117.6 12.8 %collective-permute-done.6 = f32[2,640,128]{1,2,0:T(8,128)S(1)} collective-permute-done((f32[2,640,128]{1,2,0:T(8,128)S(1)}, f32[2,640,128]{1,2,0:T(8,128)S(1)}, u32[]{:S(2)}, u32[]{:S(2)}) %collective-permute-start.6) | collective-permute-done | bytes 655392 | tf_op jit(solution)/shard_map/ppermute | solution.py:22
  135.6 9.1 %all_to_all.42 = f32[4,2,32,256]{3,2,1,0:T(8,128)S(1)} all-to-all(f32[4,2,32,256]{3,2,1,0:T(8,128)S(1)} %copy.97), channel_id=1, replica_groups=mesh['gx_0'=8,'gx_1'=2,'gy'=4,'ma'=4] {'ma'}, dimensions={0} | all-to-all | bytes 524288 | tf_op jit(solution)/shard_map/all_to_all | solution.py:46
  144.7 9.1 %all_to_all.40 = f32[4,2,32,256]{3,2,1,0:T(8,128)S(1)} all-to-all(f32[4,2,32,256]{3,2,1,0:T(8,128)S(1)} %broadcast_in_dim.24), channel_id=1, replica_groups=mesh['gx_0'=8,'gx_1'=2,'gy'=4,'ma'=4] {'ma'}, dimensions={0} | all-to-all | bytes 524288 | tf_op jit(solution)/shard_map/all_to_all | solution.py:32
  155.7 4.9 collective-permute-start.9
  170.5 7.2 %collective-permute-done.10 = f32[2,384,128]{2,1,0:T(8,128)S(1)} collective-permute-done((f32[2,384,128]{2,1,0:T(8,128)S(1)}, f32[2,384,128]{2,1,0:T(8,128)S(1)}, u32[]{:S(2)}, u32[]{:S(2)}) %collective-permute-start.10) | collective-permute-done | bytes 393248 | tf_op jit(solution)/shard_map/ppermute | solution.py:22
  189.3 5.7 bitcast_multiply_fusion.2
  205.3 23.6 %all-to-all-done.3 = f32[4,2,256,256]{3,2,1,0:T(8,128)} async-done(((f32[4,2,256,256]{3,2,1,0:T(8,128)}), f32[4,2,256,256]{3,2,1,0:T(8,128)}, u32[]{:S(2)}, u32[]{:S(2)}) %all-to-all-start.3) | async-done | bytes 2097184 | tf_op jit(solution)/shard_map/all_to_all | solution.py:32
  243.3 125.7 %psum.14 = f32[2]{0:T(128)S(1)} all-reduce(f32[2]{0:T(128)S(1)} %pad_maximum_fusion.28), channel_id=1, replica_groups=mesh['gx_0'=8,'gx_1'=2,'gy'=4,'ma'=4] {'gx_0','gx_1','gy'}, use_global_device_ids=true, to_apply=%region_9.10 | all-reduce | flops 2 | bytes 16 | tf_op jit(solution)/shard_map/psum | solution.py:226
  383.9 7.9 %dynamic_update_slice.14 = f32[2,384,512]{1,2,0:T(8,128)S(1)} dynamic-update-slice(f32[2,384,512]{1,2,0:T(8,128)S(1)} %broadcast.160, f32[2,256,256]{1,2,0:T(8,128)} %fusion.30, s32[]{:T(128)} %constant.12.clone.1, s32[]{:T(128)S(6)} %select_n.53, s32[]{:T(128)S(6)} %select_n.54) | dynamic-update-slice | bytes 1048580 | tf_op jit(solution)/shard_map/dynamic_update_slice | solution.py:201
  393.8 7.1 %dynamic_update_slice.15 = f32[2,384,512]{1,2,0:T(8,128)S(1)} dynamic-update-slice(f32[2,384,512]{1,2,0:T(8,128)S(1)} %dynamic_update_slice.14, f32[2,256,256]{1,2,0:T(8,128)} %fusion.39, s32[]{:T(128)} %constant.12.clone.1, s32[]{:T(128)S(6)} %select_n.55, s32[]{:T(128)S(6)} %select_n.56) | dynamic-update-slice | bytes 1048580 | tf_op jit(solution)/shard_map/dynamic_update_slice | solution.py:201
  402.9 4.9 collective-permute-start.13
  407.7 4.9 collective-permute-done.12
  418.5 7.8 %collective-permute-done.14 = f32[2,640,128]{1,2,0:T(8,128)S(1)} collective-permute-done((f32[2,640,128]{1,2,0:T(8,128)S(1)}, f32[2,640,128]{1,2,0:T(8,128)S(1)}, u32[]{:S(2)}, u32[]{:S(2)}) %collective-permute-start.14) | collective-permute-done | bytes 655392 | tf_op jit(solution)/shard_map/ppermute | solution.py:22
  430.9 12.1 %all_to_all.43 = f32[4,2,32,256]{3,2,1,0:T(8,128)S(1)} all-to-all(f32[4,2,32,256]{3,2,1,0:T(8,128)S(1)} %copy.108), channel_id=1, replica_groups=mesh['gx_0'=8,'gx_1'=2,'gy'=4,'ma'=4] {'ma'}, dimensions={0} | all-to-all | bytes 524288 | tf_op jit(solution)/shard_map/all_to_all | solution.py:46
  443.0 9.1 %all_to_all.41 = f32[4,2,32,256]{3,2,1,0:T(8,128)S(1)} all-to-all(f32[4,2,32,256]{3,2,1,0:T(8,128)S(1)} %broadcast_in_dim.27), channel_id=1, replica_groups=mesh['gx_0'=8,'gx_1'=2,'gy'=4,'ma'=4] {'ma'}, dimensions={0} | all-to-all | bytes 524288 | tf_op jit(solution)/shard_map/all_to_all | solution.py:32
  454.0 4.9 collective-permute-start.17
  484.4 19.5 %all-to-all-done.7 = f32[4,2,256,256]{3,2,1,0:T(8,128)S(1)} async-done(((f32[4,2,256,256]{3,2,1,0:T(8,128)}), f32[4,2,256,256]{3,2,1,0:T(8,128)S(1)}, u32[]{:S(2)}, u32[]{:S(2)}) %all-to-all-start.7) | async-done | bytes 2097184 | tf_op jit(solution)/shard_map/all_to_all | solution.py:32
  506.1 131.8 %psum.15 = f32[2]{0:T(128)S(1)} all-reduce(f32[2]{0:T(128)S(1)} %pad_maximum_fusion.29), channel_id=1, replica_groups=mesh['gx_0'=8,'gx_1'=2,'gy'=4,'ma'=4] {'gx_0','gx_1','gy'}, use_global_device_ids=true, to_apply=%region_19.20 | all-reduce | flops 2 | bytes 16 | tf_op jit(solution)/shard_map/psum | solution.py:226
  (183 shorter events, 167.0 us)
Async XLA Ops:
  0.0 9.2 %collective-permute-start = (f32[2,128,256]{2,1,0:T(8,128)}, f32[2,128,256]{2,1,0:T(8,128)S(1)}, u32[]{:S(2)}, u32[]{:S(2)}) collective-permute-start(f32[2,128,256]{2,1,0:T(8,128)} %param.5), channel_id=1, source_target_pairs={{0,16},{16,32},{32,48},{48,64},{64,80},{80,96},{96,112},{112,128},... | collective-permute-start | bytes 786440 | tf_op jit(solution)/shard_map/ppermute | solution.py:22
  2.1 9.0 %collective-permute-start.1 = (f32[2,128,256]{2,1,0:T(8,128)}, f32[2,128,256]{2,1,0:T(8,128)S(1)}, u32[]{:S(2)}, u32[]{:S(2)}) collective-permute-start(f32[2,128,256]{2,1,0:T(8,128)} %param.5), channel_id=1, source_target_pairs={{16,0},{32,16},{48,32},{64,48},{80,64},{96,80},{112,96},{128,112},... | collective-permute-start | bytes 786440 | tf_op jit(solution)/shard_map/ppermute | solution.py:25
  11.9 17.3 %collective-permute-start.2 = (f32[2,384,128]{2,1,0:T(8,128)}, f32[2,384,128]{2,1,0:T(8,128)S(1)}, u32[]{:S(2)}, u32[]{:S(2)}) collective-permute-start(f32[2,384,128]{2,1,0:T(8,128)} %get-tuple-element.45), channel_id=1, source_target_pairs={{0,4},{4,8},{8,12},{1,5},{5,9},{9,13},{2,6},{6,10},{10,14},{3,7},{... | collective-permute-start | bytes 1179656 | tf_op jit(solution)/shard_map/ppermute | solution.py:22
  15.4 13.8 %collective-permute-start.3 = (f32[2,384,128]{2,1,0:T(8,128)S(1)}, f32[2,384,128]{2,1,0:T(8,128)S(1)}, u32[]{:S(2)}, u32[]{:S(2)}) collective-permute-start(f32[2,384,128]{2,1,0:T(8,128)S(1)} %get-tuple-element.46), channel_id=1, source_target_pairs={{4,0},{8,4},{12,8},{5,1},{9,5},{13,9},{6,2},{10,6},{14,10},{7,3},{... | collective-permute-start | bytes 1179656 | tf_op jit(solution)/shard_map/ppermute | solution.py:25
  39.8 31.0 %all-to-all-start = ((f32[4,2,256,256]{3,2,1,0:T(8,128)}), f32[4,2,256,256]{3,2,1,0:T(8,128)}, u32[]{:S(2)}, u32[]{:S(2)}) async-start(f32[4,2,256,256]{3,2,1,0:T(8,128)} %broadcast_in_dim.23), calls=%async_computation | async-start | bytes 4194304 | tf_op jit(solution)/shard_map/all_to_all | solution.py:32
  98.3 11.7 %collective-permute-start.4 = (f32[2,128,512]{1,2,0:T(8,128)S(1)}, f32[2,128,512]{1,2,0:T(8,128)S(1)}, u32[]{:S(2)}, u32[]{:S(2)}) collective-permute-start(f32[2,128,512]{1,2,0:T(8,128)S(1)} %get-tuple-element.29), channel_id=1, source_target_pairs={{0,16},{16,32},{32,48},{48,64},{64,80},{80,96},{96,112},{112,128},... | collective-permute-start | bytes 1572872 | tf_op jit(solution)/shard_map/ppermute | solution.py:22
  100.2 11.5 %collective-permute-start.5 = (f32[2,128,512]{1,2,0:T(8,128)S(1)}, f32[2,128,512]{1,2,0:T(8,128)S(1)}, u32[]{:S(2)}, u32[]{:S(2)}) collective-permute-start(f32[2,128,512]{1,2,0:T(8,128)S(1)} %get-tuple-element.30), channel_id=1, source_target_pairs={{16,0},{32,16},{48,32},{64,48},{80,64},{96,80},{112,96},{128,112},... | collective-permute-start | bytes 1572872 | tf_op jit(solution)/shard_map/ppermute | solution.py:25
  111.8 18.6 %collective-permute-start.6 = (f32[2,640,128]{1,2,0:T(8,128)S(1)}, f32[2,640,128]{1,2,0:T(8,128)S(1)}, u32[]{:S(2)}, u32[]{:S(2)}) collective-permute-start(f32[2,640,128]{1,2,0:T(8,128)S(1)} %get-tuple-element.13), channel_id=1, source_target_pairs={{0,4},{4,8},{8,12},{1,5},{5,9},{9,13},{2,6},{6,10},{10,14},{3,7},{... | collective-permute-start | bytes 1966088 | tf_op jit(solution)/shard_map/ppermute | solution.py:22
  116.3 18.3 %collective-permute-start.7 = (f32[2,640,128]{1,2,0:T(8,128)S(1)}, f32[2,640,128]{1,2,0:T(8,128)S(1)}, u32[]{:S(2)}, u32[]{:S(2)}) collective-permute-start(f32[2,640,128]{1,2,0:T(8,128)S(1)} %get-tuple-element.14), channel_id=1, source_target_pairs={{4,0},{8,4},{12,8},{5,1},{9,5},{13,9},{6,2},{10,6},{14,10},{7,3},{... | collective-permute-start | bytes 1966088 | tf_op jit(solution)/shard_map/ppermute | solution.py:25
  153.8 8.9 %collective-permute-start.8 = (f32[2,128,256]{2,1,0:T(8,128)S(1)}, f32[2,128,256]{2,1,0:T(8,128)S(1)}, u32[]{:S(2)}, u32[]{:S(2)}) collective-permute-start(f32[2,128,256]{2,1,0:T(8,128)S(1)} %bitcast.294), channel_id=1, source_target_pairs={{0,16},{16,32},{32,48},{48,64},{64,80},{80,96},{96,112},{112,128},... | collective-permute-start | bytes 786440 | tf_op jit(solution)/shard_map/ppermute | solution.py:22
  155.7 8.7 %collective-permute-start.9 = (f32[2,128,256]{2,1,0:T(8,128)S(1)}, f32[2,128,256]{2,1,0:T(8,128)S(1)}, u32[]{:S(2)}, u32[]{:S(2)}) collective-permute-start(f32[2,128,256]{2,1,0:T(8,128)S(1)} %bitcast.295), channel_id=1, source_target_pairs={{16,0},{32,16},{48,32},{64,48},{80,64},{96,80},{112,96},{128,112},... | collective-permute-start | bytes 786440 | tf_op jit(solution)/shard_map/ppermute | solution.py:25
  164.5 13.2 %collective-permute-start.10 = (f32[2,384,128]{2,1,0:T(8,128)S(1)}, f32[2,384,128]{2,1,0:T(8,128)S(1)}, u32[]{:S(2)}, u32[]{:S(2)}) collective-permute-start(f32[2,384,128]{2,1,0:T(8,128)S(1)} %get-tuple-element.43), channel_id=1, source_target_pairs={{0,4},{4,8},{8,12},{1,5},{5,9},{9,13},{2,6},{6,10},{10,14},{3,7},{... | collective-permute-start | bytes 1179656 | tf_op jit(solution)/shard_map/ppermute | solution.py:22
  169.1 13.1 %collective-permute-start.11 = (f32[2,384,128]{2,1,0:T(8,128)S(1)}, f32[2,384,128]{2,1,0:T(8,128)S(1)}, u32[]{:S(2)}, u32[]{:S(2)}) collective-permute-start(f32[2,384,128]{2,1,0:T(8,128)S(1)} %get-tuple-element.44), channel_id=1, source_target_pairs={{4,0},{8,4},{12,8},{5,1},{9,5},{13,9},{6,2},{10,6},{14,10},{7,3},{... | collective-permute-start | bytes 1179656 | tf_op jit(solution)/shard_map/ppermute | solution.py:25
  198.3 30.6 %all-to-all-start.3 = ((f32[4,2,256,256]{3,2,1,0:T(8,128)}), f32[4,2,256,256]{3,2,1,0:T(8,128)}, u32[]{:S(2)}, u32[]{:S(2)}) async-start(f32[4,2,256,256]{3,2,1,0:T(8,128)} %broadcast_in_dim.25), calls=%async_computation.3 | async-start | bytes 4194304 | tf_op jit(solution)/shard_map/all_to_all | solution.py:32
  231.4 140.3 %all-to-all-start.4 = ((f32[4,2,256,256]{3,2,1,0:T(8,128)}), f32[4,2,256,256]{3,2,1,0:T(8,128)}, u32[]{:S(2)}, u32[]{:S(2)}) async-start(f32[4,2,256,256]{3,2,1,0:T(8,128)} %broadcast_in_dim.26), calls=%async_computation.4 | async-start | bytes 4194304 | tf_op jit(solution)/shard_map/all_to_all | solution.py:32
  400.9 11.7 %collective-permute-start.12 = (f32[2,128,512]{1,2,0:T(8,128)S(1)}, f32[2,128,512]{1,2,0:T(8,128)S(1)}, u32[]{:S(2)}, u32[]{:S(2)}) collective-permute-start(f32[2,128,512]{1,2,0:T(8,128)S(1)} %get-tuple-element.25), channel_id=1, source_target_pairs={{0,16},{16,32},{32,48},{48,64},{64,80},{80,96},{96,112},{112,128},... | collective-permute-start | bytes 1572872 | tf_op jit(solution)/shard_map/ppermute | solution.py:22
  402.9 11.5 %collective-permute-start.13 = (f32[2,128,512]{1,2,0:T(8,128)S(1)}, f32[2,128,512]{1,2,0:T(8,128)S(1)}, u32[]{:S(2)}, u32[]{:S(2)}) collective-permute-start(f32[2,128,512]{1,2,0:T(8,128)S(1)} %get-tuple-element.26), channel_id=1, source_target_pairs={{16,0},{32,16},{48,32},{64,48},{80,64},{96,80},{112,96},{128,112},... | collective-permute-start | bytes 1572872 | tf_op jit(solution)/shard_map/ppermute | solution.py:25
  414.5 11.8 %collective-permute-start.14 = (f32[2,640,128]{1,2,0:T(8,128)S(1)}, f32[2,640,128]{1,2,0:T(8,128)S(1)}, u32[]{:S(2)}, u32[]{:S(2)}) collective-permute-start(f32[2,640,128]{1,2,0:T(8,128)S(1)} %get-tuple-element.11), channel_id=1, source_target_pairs={{0,4},{4,8},{8,12},{1,5},{5,9},{9,13},{2,6},{6,10},{10,14},{3,7},{... | collective-permute-start | bytes 1966088 | tf_op jit(solution)/shard_map/ppermute | solution.py:22
  417.2 13.2 %collective-permute-start.15 = (f32[2,640,128]{1,2,0:T(8,128)S(1)}, f32[2,640,128]{1,2,0:T(8,128)S(1)}, u32[]{:S(2)}, u32[]{:S(2)}) collective-permute-start(f32[2,640,128]{1,2,0:T(8,128)S(1)} %get-tuple-element.12), channel_id=1, source_target_pairs={{4,0},{8,4},{12,8},{5,1},{9,5},{13,9},{6,2},{10,6},{14,10},{7,3},{... | collective-permute-start | bytes 1966088 | tf_op jit(solution)/shard_map/ppermute | solution.py:25
  452.1 8.9 %collective-permute-start.16 = (f32[2,128,256]{2,1,0:T(8,128)S(1)}, f32[2,128,256]{2,1,0:T(8,128)S(1)}, u32[]{:S(2)}, u32[]{:S(2)}) collective-permute-start(f32[2,128,256]{2,1,0:T(8,128)S(1)} %bitcast.298), channel_id=1, source_target_pairs={{0,16},{16,32},{32,48},{48,64},{64,80},{80,96},{96,112},{112,128},... | collective-permute-start | bytes 786440 | tf_op jit(solution)/shard_map/ppermute | solution.py:22
  454.0 8.7 %collective-permute-start.17 = (f32[2,128,256]{2,1,0:T(8,128)S(1)}, f32[2,128,256]{2,1,0:T(8,128)S(1)}, u32[]{:S(2)}, u32[]{:S(2)}) collective-permute-start(f32[2,128,256]{2,1,0:T(8,128)S(1)} %bitcast.299), channel_id=1, source_target_pairs={{16,0},{32,16},{48,32},{64,48},{80,64},{96,80},{112,96},{128,112},... | collective-permute-start | bytes 786440 | tf_op jit(solution)/shard_map/ppermute | solution.py:25
  462.9 7.2 %collective-permute-start.18 = (f32[2,384,128]{2,1,0:T(8,128)S(1)}, f32[2,384,128]{2,1,0:T(8,128)S(1)}, u32[]{:S(2)}, u32[]{:S(2)}) collective-permute-start(f32[2,384,128]{2,1,0:T(8,128)S(1)} %get-tuple-element.41), channel_id=1, source_target_pairs={{0,4},{4,8},{8,12},{1,5},{5,9},{9,13},{2,6},{6,10},{10,14},{3,7},{... | collective-permute-start | bytes 1179656 | tf_op jit(solution)/shard_map/ppermute | solution.py:22
  464.8 9.7 %collective-permute-start.19 = (f32[2,384,128]{2,1,0:T(8,128)S(1)}, f32[2,384,128]{2,1,0:T(8,128)S(1)}, u32[]{:S(2)}, u32[]{:S(2)}) collective-permute-start(f32[2,384,128]{2,1,0:T(8,128)S(1)} %get-tuple-element.42), channel_id=1, source_target_pairs={{4,0},{8,4},{12,8},{5,1},{9,5},{13,9},{6,2},{10,6},{14,10},{7,3},{... | collective-permute-start | bytes 1179656 | tf_op jit(solution)/shard_map/ppermute | solution.py:25
  480.0 23.9 %all-to-all-start.7 = ((f32[4,2,256,256]{3,2,1,0:T(8,128)}), f32[4,2,256,256]{3,2,1,0:T(8,128)S(1)}, u32[]{:S(2)}, u32[]{:S(2)}) async-start(f32[4,2,256,256]{3,2,1,0:T(8,128)} %broadcast_in_dim.28), calls=%async_computation.7 | async-start | bytes 4194304 | tf_op jit(solution)/shard_map/all_to_all | solution.py:32
  (22 other events, 440.9 us)

commit v2 on v1

v2 whole, which is shorter than its diff:
```python
import functools
import math

import jax
import jax.numpy as jnp
import numpy as np
from jax import lax
from jax.experimental import pallas as pl
from jax.experimental.pallas import tpu as pltpu
from jax.sharding import PartitionSpec as P

OUTER = 2
DAMPING = 1.0
MESH = pl.DeviceIdType.MESH
F32 = jnp.float32
BF16 = jnp.bfloat16


def dft_parts(n):
    ladder = np.arange(n, dtype=np.int32)
    phases = ladder[:, None] * ladder[None, :] % n
    angles = phases.astype(np.float32) * np.float32(2.0 * math.pi / n)
    factor = np.float32(1.0 / math.sqrt(n))
    return np.stack([np.cos(angles) * factor, -np.sin(angles) * factor]).astype(BF16)


class Copies:
    def __init__(self, send_sems, recv_sems):
        self.send_sems, self.recv_sems, self.count, self.pending = send_sems, recv_sems, 0, []

    def make(self, src, dst, device, sends=None):
        copy = pltpu.make_async_remote_copy(
            src_ref=src,
            dst_ref=dst,
            send_sem=self.send_sems.at[self.count],
            recv_sem=self.recv_sems.at[self.count],
            device_id=device,
            device_id_type=MESH,
        )
        self.count += 1
        self.pending.append((copy, sends))
        return copy

    def finish(self):
        for copy, sends in self.pending:
            when(sends, copy.wait_send)
        self.pending = []


def when(condition, action):
    if condition is None:
        action()
    else:
        pl.when(condition)(action)


def kernel(
    dims,
    obj_hbm,
    probe_hbm,
    meas_hbm,
    pos_ref,
    count_ref,
    w_ref,
    out_ref,
    obj,
    cur,
    probes,
    meas,
    t_one,
    t_two,
    t_back,
    t_three,
    win,
    wave,
    half,
    spec,
    moved,
    turned,
    weight,
    placed,
    cut_rows,
    cut_cols,
    put_rows,
    put_cols,
    terms_a,
    terms_b,
    terms_c,
    terms_d,
    ext,
    dirs,
    from_z,
    from_y,
    from_ma,
    sums_ma,
    sums_gy,
    sums_gx,
    local_sems,
    send_sems,
    recv_sems,
):
    n_gx, n_gy, n_ma, n, tx, ty = dims
    rim = n // 2
    kh = n // 2
    gx, gy, ma = lax.axis_index("gx"), lax.axis_index("gy"), lax.axis_index("ma")
    core = lax.rem(gx, 2)
    slot, part_k = ma // 2, lax.rem(ma, 2)
    up, down = gx > 0, gx < n_gx - 1
    left, right = gy > 0, gy < n_gy - 1
    copies = Copies(send_sems, recv_sems)
    terms = (terms_a, terms_b, terms_c, terms_d)

    barrier = pltpu.get_barrier_semaphore()
    for axis, size, me in (("gx", n_gx, gx), ("gy", n_gy, gy), ("ma", n_ma, ma)):
        for o in range(1, size):
            pl.semaphore_signal(
                barrier, inc=1, device_id={axis: lax.rem(me + o, size)}, device_id_type=MESH
            )

    k_rows = pl.ds(pl.multiple_of(part_k * kh, kh), kh)
    own_rows, own_cols = pl.ds(rim, tx), pl.ds(rim, ty)
    loads = [
        pltpu.make_async_copy(obj_hbm, cur.at[:, own_rows, own_cols], local_sems.at[0]),
        pltpu.make_async_copy(obj_hbm, obj, local_sems.at[1]),
        pltpu.make_async_copy(probe_hbm, probes.at[0], local_sems.at[2]),
        pltpu.make_async_copy(meas_hbm.at[0, 0, slot, k_rows], meas, local_sems.at[3]),
    ]
    for load in loads:
        load.start()

    w_re, w_im = w_ref[0], w_ref[1]
    t_two[:n, :n], t_two[:n, n:], t_two[n:, :n], t_two[n:, n:] = w_re, w_im, -w_im, w_re
    t_back[:n, :n], t_back[:n, n:], t_back[n:, :n], t_back[n:, n:] = w_re, -w_im, w_im, w_re
    wk_re, wk_im = w_ref[0, k_rows, :], w_ref[1, k_rows, :]
    t_one[:kh, :n], t_one[:kh, n:], t_one[kh:, :n], t_one[kh:, n:] = wk_re, -wk_im, wk_im, wk_re
    k_cols = pl.ds(pl.multiple_of(part_k * kh, kh), kh)
    wc_re, wc_im = w_ref[0, :, k_cols], w_ref[1, :, k_cols]
    t_three[:n, :kh], t_three[:n, kh:] = wc_re, wc_im
    t_three[n:, :kh], t_three[n:, kh:] = -wc_im, wc_re

    def clear(ref):
        ref[...] = jnp.zeros(ref.shape, ref.dtype)

    padded = [cur] + [dirs.at[it] for it in range(OUTER)]
    for p in range(2):
        for buf in padded:
            when(gx == 0, functools.partial(clear, buf.at[p, pl.ds(0, rim)]))
            when(gx == n_gx - 1, functools.partial(clear, buf.at[p, pl.ds(rim + tx, rim)]))
            when(gy == 0, functools.partial(clear, buf.at[p, own_rows, pl.ds(0, rim)]))
            when(gy == n_gy - 1, functools.partial(clear, buf.at[p, own_rows, pl.ds(rim + ty, rim)]))
        for it in range(OUTER):
            when(gx == n_gx - 1, functools.partial(clear, from_z.at[it, 0, p]))
            when(gx == 0, functools.partial(clear, from_z.at[it, 1, p]))
            when(gy == n_gy - 1, functools.partial(clear, from_y.at[it, 0, p]))
            when(gy == 0, functools.partial(clear, from_y.at[it, 1, p]))

    for load in loads:
        load.wait()
    pl.semaphore_wait(barrier, n_gx + n_gy + n_ma - 3)

    ma_next, ma_prev = {"ma": lax.rem(ma + 1, n_ma)}, {"ma": lax.rem(ma + n_ma - 1, n_ma)}
    partner = {"gx": gx + 1 - 2 * core}
    ring = {}
    for part, other in ((0, 1), (1, 0)):
        ring["n", part] = copies.make(probes.at[0, core, part], probes.at[1, core, part], ma_next)
        ring["p", other] = copies.make(probes.at[0, core, other], probes.at[3, core, other], ma_prev)
        ring["n", part].start()
        ring["p", other].start()

    def shift_y(buf, p):
        low = copies.make(
            buf.at[p, own_rows, pl.ds(rim, rim)],
            buf.at[p, own_rows, pl.ds(rim + ty, rim)],
            {"gy": gy - 1},
            left,
        )
        high = copies.make(
            buf.at[p, own_rows, pl.ds(ty, rim)],
            buf.at[p, own_rows, pl.ds(0, rim)],
            {"gy": gy + 1},
            right,
        )
        when(left, low.start)
        when(right, high.start)
        return ((right, low), (left, high))

    def shift_x(buf, p):
        low = copies.make(
            buf.at[p, own_rows], buf.at[p, pl.ds(rim + tx, rim)], {"gx": gx - 1}, up
        )
        high = copies.make(buf.at[p, own_rows], buf.at[p, pl.ds(0, rim)], {"gx": gx + 1}, down)
        when(up, low.start)
        when(down, high.start)
        return ((down, low), (up, high))

    def arrive(arrivals):
        for condition, copy in arrivals:
            when(condition, copy.wait_recv)

    def widen(buf):
        beside = [shift_y(buf, p) for p in range(2)]
        return beside

    def widen_end(buf, beside):
        stacked = []
        for p in range(2):
            arrive(beside[p])
            stacked.append(shift_x(buf, p))
        for p in range(2):
            arrive(stacked[p])

    widen_end(cur, widen(cur))

    row_at, col_at = pos_ref[0, 0, slot, 0], pos_ref[0, 0, slot, 1]
    live = jnp.where(slot < count_ref[0, 0], 1.0, 0.0).astype(F32)
    tall, width = 2 * rim + tx, 2 * rim + ty

    def chosen(shape, dim, first):
        here = lax.broadcasted_iota(jnp.int32, shape, dim)
        there = lax.broadcasted_iota(jnp.int32, shape, 1 - dim)
        return jnp.where(here == there + first, 1.0, 0.0).astype(BF16)

    for i in range(2):
        cut_rows[:, i * tall : (i + 1) * tall] = chosen((n, tall), 1, row_at)
        cut_cols[i * width : (i + 1) * width] = chosen((width, n), 0, col_at)
        put_rows[:, i * n : (i + 1) * n] = chosen((tall, n), 0, row_at)
        put_cols[i * n : (i + 1) * n] = chosen((n, width), 1, col_at)

    def two_terms(x, ref, axis):
        top = x.astype(BF16)
        rest = (x - top.astype(F32)).astype(BF16)
        size = x.shape[axis]
        if axis == 0:
            ref[:size], ref[size:] = top, rest
        else:
            ref[:, :size], ref[:, size:] = top, rest
        return ref[...]

    def dot(x, y):
        return jnp.dot(x, y, preferred_element_type=F32)

    def window(buf):
        def cut(p, _):
            x = dot(two_terms(buf[p], terms[0], 1), cut_cols[...])
            win[p] = dot(cut_rows[...], two_terms(x, terms[1], 0))
            return 0

        lax.fori_loop(0, 2, cut, 0)

    def forward_pair(d):
        for c in range(2):
            pr, pi = probes[d, c, 0], probes[d, c, 1]
            wr, wi = win[0], win[1]
            wave[c, :n] = (pr * wr - pi * wi).astype(BF16)
            wave[c, n:] = (pr * wi + pi * wr).astype(BF16)
            h = dot(t_one[...], wave[c]).astype(BF16)
            half[c * kh : (c + 1) * kh, :n] = h[:kh]
            half[c * kh : (c + 1) * kh, n:] = h[kh:]
        return dot(half[...], t_two[...])

    def pair_rows(d):
        return pl.ds(pl.multiple_of(d * n, n), n)

    def folded(x):
        x = x[:kh] + x[kh:]
        return x[:, :n] + x[:, n:]

    def backward(misfit):
        weight[:, :n] = 2.0 * misfit
        weight[:, n:] = 2.0 * misfit

        def pair(d, _):
            y = weight[...]
            f = spec[pair_rows(d), :]
            half[:kh] = (f[:kh] * y).astype(BF16)
            half[kh:] = (f[kh:] * y).astype(BF16)
            b = dot(half[...], t_back[...]).astype(BF16)
            for c in range(2):
                turned[c, :kh] = b[c * kh : (c + 1) * kh, :n]
                turned[c, kh:] = b[c * kh : (c + 1) * kh, n:]
                g = dot(t_three[...], turned[c])
                pr, pi = probes[d, c, 0], probes[d, c, 1]
                placed[0] += pr * g[:n] + pi * g[n:]
                placed[1] += pr * g[n:] - pi * g[:n]
            return 0

        clear(placed)
        lax.fori_loop(0, n_ma, pair, 0)

    def place(it):
        def put(q, _):
            x = dot(put_rows[...], two_terms(placed[q], terms[2], 0))
            ext[it, q] = dot(two_terms(x, terms[3], 1), put_cols[...])
            return 0

        lax.fori_loop(0, 2, put, 0)

    quarter = tx // n_ma
    my_quarter = pl.ds(pl.multiple_of(rim + ma * quarter, quarter), quarter)

    def combine(it):
        place(it)
        sent = []
        for p in range(2):
            low = copies.make(
                ext.at[it, p, pl.ds(0, rim)], from_z.at[it, 0, p], {"gx": gx - 1}, up
            )
            high = copies.make(
                ext.at[it, p, pl.ds(rim + tx, rim)], from_z.at[it, 1, p], {"gx": gx + 1}, down
            )
            when(up, low.start)
            when(down, high.start)
            sent.append(((down, low), (up, high)))
        beside = []
        for p in range(2):
            arrive(sent[p])
            ext[it, p, own_rows] += from_z[it, 0, p] + from_z[it, 1, p]
            low = copies.make(
                ext.at[it, p, own_rows, pl.ds(0, rim)], from_y.at[it, 0, p], {"gy": gy - 1}, left
            )
            high = copies.make(
                ext.at[it, p, own_rows, pl.ds(rim + ty, rim)],
                from_y.at[it, 1, p],
                {"gy": gy + 1},
                right,
            )
            when(left, low.start)
            when(right, high.start)
            beside.append(((right, low), (left, high)))
        quarters = []
        for p in range(2):
            arrive(beside[p])
            ext[it, p, own_rows, pl.ds(ty, rim)] += from_y[it, 0, p]
            ext[it, p, own_rows, pl.ds(rim, rim)] += from_y[it, 1, p]
            batch = []
            for o in range(1, n_ma):
                peer = lax.rem(ma + o, n_ma)
                rows = pl.ds(pl.multiple_of(rim + peer * quarter, quarter), quarter)
                copy = copies.make(
                    ext.at[it, p, rows, own_cols], from_ma.at[it, o - 1, p], {"ma": peer}
                )
                copy.start()
                batch.append(copy)
            quarters.append(batch)
        gathers, square = [], jnp.zeros((8, 128), F32)
        for p in range(2):
            total = ext[it, p, my_quarter, own_cols]
            for o in range(1, n_ma):
                quarters[p][o - 1].wait_recv()
                total += from_ma[it, o - 1, p]
            dirs[it, p, my_quarter, own_cols] = -total
            square += squares(total)
            batch = []
            for o in range(1, n_ma):
                mine = dirs.at[it, p, my_quarter, own_cols]
                copy = copies.make(mine, mine, {"ma": lax.rem(ma + o, n_ma)})
                copy.start()
                batch.append(copy)
            gathers.append(batch)
        beside = []
        for p in range(2):
            for copy in gathers[p]:
                copy.wait_recv()
            beside.append(shift_y(dirs.at[it], p))
        widen_end(dirs.at[it], beside)
        return square

    def squares(x):
        x = x * x
        out = x[:, :128]
        for i in range(1, x.shape[1] // 128):
            out = out + x[:, i * 128 : (i + 1) * 128]
        return jnp.sum(out.reshape(-1, 8, 128), axis=0)

    def step_size(it, square, changes):
        value = jnp.stack([square, changes])
        for axis, size, me, buf in (
            ("ma", n_ma, ma, sums_ma),
            ("gy", n_gy, gy, sums_gy),
            ("gx", n_gx, gx, sums_gx),
        ):
            buf[it, me] = value
            batch = []
            for o in range(1, size):
                mine = buf.at[it, me]
                copy = copies.make(mine, mine, {axis: lax.rem(me + o, size)})
                copy.start()
                batch.append(copy)
            for copy in batch:
                copy.wait_recv()
            value = buf[it, 0]
            for i in range(1, size):
                value += buf[it, i]
        norm = jnp.sum(value[0], keepdims=True)
        return norm / (jnp.sum(value[1], keepdims=True) + DAMPING * norm)

    window(cur)
    intensity = jnp.zeros((kh, n), F32)

    def hand(d, part):
        copy = copies.make(probes.at[d, core, part], probes.at[d, core, part], partner)
        copy.start()
        return copy

    handed = {}
    for part, other in ((0, 1), (1, 0)):
        ring["n", part].wait_recv()
        ring["p", other].wait_recv()
        if part == 0:
            forth = copies.make(probes.at[1, core, 0], probes.at[2, core, 0], ma_next)
            back = copies.make(probes.at[3, core, 1], probes.at[2, core, 1], ma_prev)
            forth.start()
            back.start()
        handed[1, part] = hand(1, part)
        handed[3, other] = hand(3, other)
        if part == 0:
            f = forward_pair(0)
            spec[pair_rows(0), :] = f
            intensity += folded(f * f)
    for d in (1, 3):
        handed[d, 0].wait_recv()
        handed[d, 1].wait_recv()
        f = forward_pair(d)
        spec[pair_rows(d), :] = f
        intensity += folded(f * f)
    forth.wait_recv()
    handed[2, 0] = hand(2, 0)
    back.wait_recv()
    handed[2, 1] = hand(2, 1)
    handed[2, 0].wait_recv()
    handed[2, 1].wait_recv()
    f = forward_pair(2)
    spec[pair_rows(2), :] = f
    intensity += folded(f * f)

    for it in range(OUTER):
        backward(live * (intensity - meas[...]))
        square = combine(it)
        window(dirs.at[it])
        last = it + 1 == OUTER

        def pair(d, change, last=last):
            m = forward_pair(d)
            if not last:
                moved[pair_rows(d), :] = m
            return change + folded(spec[pair_rows(d), :] * m)

        change = live * 2.0 * lax.fori_loop(0, n_ma, pair, jnp.zeros((kh, n), F32))
        alpha = step_size(it, square, squares(change))
        obj[...] += alpha * dirs[it, :, own_rows, own_cols]
        if not last:

            def advance(d, total, alpha=alpha):
                f = spec[pair_rows(d), :] + alpha * moved[pair_rows(d), :]
                spec[pair_rows(d), :] = f
                return total + folded(f * f)

            intensity = lax.fori_loop(0, n_ma, advance, jnp.zeros((kh, n), F32))
    out_ref[...] = obj[...]
    copies.finish()


def solution(mesh):
    sizes = (mesh.shape["gx"], mesh.shape["gy"], mesh.shape["ma"])

    def shards(object_field, probe_modes, measured, positions, slot_counts):
        n = probe_modes.shape[-1]
        _, tx, ty = object_field.shape
        rim, kh = n // 2, n // 2
        wide = (2, tx + 2 * rim, ty + 2 * rim)
        modes = probe_modes.shape[0] * sizes[2]
        quarter = tx // sizes[2]
        vmem = pltpu.VMEM
        scratch = [
            vmem((2, tx, ty), F32),
            vmem(wide, F32),
            vmem((sizes[2], 2, 2, n, n), F32),
            vmem((kh, n), F32),
            vmem((n, 2 * n), BF16),
            vmem((2 * n, 2 * n), BF16),
            vmem((2 * n, 2 * n), BF16),
            vmem((2 * n, n), BF16),
            vmem((2, n, n), F32),
            vmem((2, 2 * n, n), BF16),
            vmem((n, 2 * n), BF16),
            vmem((modes * kh, 2 * n), F32),
            vmem((modes * kh, 2 * n), F32),
            vmem((2, n, n), BF16),
            vmem((kh, 2 * n), F32),
            vmem((2, n, n), F32),
            vmem((n, 2 * wide[1]), BF16),
            vmem((2 * wide[2], n), BF16),
            vmem((wide[1], 2 * n), BF16),
            vmem((2 * n, wide[2]), BF16),
            vmem((wide[1], 2 * wide[2]), BF16),
            vmem((2 * wide[1], n), BF16),
            vmem((2 * n, n), BF16),
            vmem((wide[1], 2 * n), BF16),
            vmem((OUTER, *wide), F32),
            vmem((OUTER, *wide), F32),
            vmem((OUTER, 2, 2, tx, ty + 2 * rim), F32),
            vmem((OUTER, 2, 2, tx, rim), F32),
            vmem((OUTER, sizes[2] - 1, 2, quarter, ty), F32),
            vmem((OUTER, sizes[2], 2, 8, 128), F32),
            vmem((OUTER, sizes[1], 2, 8, 128), F32),
            vmem((OUTER, sizes[0], 2, 8, 128), F32),
            pltpu.SemaphoreType.DMA((4,)),
            pltpu.SemaphoreType.DMA((128,)),
            pltpu.SemaphoreType.DMA((128,)),
        ]
        anywhere = pl.BlockSpec(memory_space=pl.ANY)
        smem = pl.BlockSpec(memory_space=pltpu.SMEM)
        in_vmem = pl.BlockSpec(memory_space=pltpu.VMEM)
        return pl.pallas_call(
            functools.partial(kernel, (*sizes, n, tx, ty)),
            out_shape=jax.ShapeDtypeStruct(object_field.shape, F32),
            in_specs=[anywhere, anywhere, anywhere, smem, smem, in_vmem],
            out_specs=in_vmem,
            scratch_shapes=scratch,
            compiler_params=pltpu.CompilerParams(
                collective_id=0, has_side_effects=True, vmem_limit_bytes=60 * 1024 * 1024
            ),
        )(object_field, probe_modes, measured, positions, slot_counts, jnp.asarray(dft_parts(n)))

    placed = (
        P(None, "gx", "gy"),
        P("ma", None, None, None),
        P("gx", "gy", None, None, None),
        P("gx", "gy", None, None),
        P("gx", "gy"),
    )
    return jax.shard_map(
        shards, mesh=mesh, in_specs=placed, out_specs=P(None, "gx", "gy"), check_vma=False
    )
```

time: 641 us -> 135 us (0.21)
  the two profiles are of different devices: /device:TPU:128 before, /device:TPU:1 now
where the time goes in v2:
time: 135 us
  Pallas kernels  132 us (98%)
  local copies, waits for them, and re-layouts  1.67 us (1%)
    pallas_call x1, Pallas kernels, shards(): pl.pallas_call(functools.partial(kernel, (*sizes, n, tx, ty)), out_shape=...  132 us

profile of v2, /device:TPU:1, one launch (start us, length us, event | category | flops | bytes accessed | tf_op | source)
XLA Modules:
  0.0 134.6 jit_solution(15908301826129077641)
XLA Ops:
  0.7 132.3 %shard_map.64 = f32[2,128,256]{2,1,0:T(8,128)} custom-call(f32[2,128,256]{2,1,0:T(8,128)} %obj_hbm.1, f32[2,2,256,256]{3,2,1,0:T(8,128)} %probe_hbm.1, f32[1,1,2,256,256]{4,3,2,1,0:T(8,128)} %meas_hbm.1, s32[1,1,2,2]{3,2,1,0:T(2,128)} %pos_ref.1, s32[1,1]{1,0:T(1,128)S(6)} %copy.8.count_ref, bf16[2,256,256]{2,1,0:T(8,128)(2,1)} %constant.2.clone.w_ref), custom_call_target="tpu_custom_call" | custom-call | tf_op jit(solution)/shard_map/pallas_call | solution.py:514
  133.0 1.7 %copy.9 = f32[2,128,256]{2,1,0:T(8,128)} copy(f32[2,128,256]{2,1,0:T(8,128)} %shard_map.64) | data formatting | bytes 524288

commit v3 on v2

v3 whole, which is shorter than its diff:
```python
import functools
import math

import jax
import jax.numpy as jnp
import numpy as np
from jax import lax
from jax.experimental import pallas as pl
from jax.experimental.pallas import tpu as pltpu
from jax.sharding import PartitionSpec as P

OUTER = 2
DAMPING = 1.0
MESH = pl.DeviceIdType.MESH
F32 = jnp.float32
BF16 = jnp.bfloat16


def dft_parts(n):
    ladder = np.arange(n, dtype=np.int32)
    phases = ladder[:, None] * ladder[None, :] % n
    angles = phases.astype(np.float32) * np.float32(2.0 * math.pi / n)
    factor = np.float32(1.0 / math.sqrt(n))
    return np.stack([np.cos(angles) * factor, -np.sin(angles) * factor]).astype(BF16)


class Copies:
    def __init__(self, send_sems, recv_sems):
        self.send_sems, self.recv_sems, self.count, self.pending = send_sems, recv_sems, 0, []

    def make(self, src, dst, device, sends=None):
        copy = pltpu.make_async_remote_copy(
            src_ref=src,
            dst_ref=dst,
            send_sem=self.send_sems.at[self.count],
            recv_sem=self.recv_sems.at[self.count],
            device_id=device,
            device_id_type=MESH,
        )
        self.count += 1
        self.pending.append((copy, sends))
        return copy

    def finish(self):
        for copy, sends in self.pending:
            when(sends, copy.wait_send)
        self.pending = []


def when(condition, action):
    if condition is None:
        action()
    else:
        pl.when(condition)(action)


def kernel(
    dims,
    obj_hbm,
    probe_hbm,
    meas_hbm,
    pos_ref,
    count_ref,
    w_ref,
    out_ref,
    obj,
    wide,
    cut,
    lent,
    probes,
    meas,
    t_one,
    t_two,
    t_back,
    t_three,
    win,
    wave,
    half,
    spec,
    moved,
    turned,
    weight,
    patch,
    tall,
    cut_rows,
    cut_cols,
    put_rows,
    put_cols,
    columns,
    terms_cols,
    terms_rows,
    terms_patch,
    terms_put,
    ext,
    from_z,
    from_y,
    from_ma,
    sums_plane,
    sums_line,
    local_sems,
    send_sems,
    recv_sems,
):
    n_gx, n_gy, n_ma, n, tx, ty = dims
    rim = n // 2
    kh = n // 2
    gx, gy, ma = lax.axis_index("gx"), lax.axis_index("gy"), lax.axis_index("ma")
    core = lax.rem(gx, 2)
    slot, part_k = ma // 2, lax.rem(ma, 2)
    up, down = gx > 0, gx < n_gx - 1
    left, right = gy > 0, gy < n_gy - 1
    copies = Copies(send_sems, recv_sems)
    row_chunk = tx // 2
    chunks = [(p, j * row_chunk) for p in range(2) for j in range(2)]

    barrier = pltpu.get_barrier_semaphore()
    line = [{"gx": lax.rem(gx + o, n_gx)} for o in range(1, n_gx)]
    plane = [
        {"gy": lax.rem(gy + o // n_ma, n_gy), "ma": lax.rem(ma + o % n_ma, n_ma)}
        for o in range(1, n_gy * n_ma)
    ]
    for device in line + plane:
        pl.semaphore_signal(barrier, inc=1, device_id=device, device_id_type=MESH)

    k_rows = pl.ds(pl.multiple_of(part_k * kh, kh), kh)
    own_cols = pl.ds(rim, ty)
    loads = [
        pltpu.make_async_copy(obj_hbm, wide.at[0, :, :, own_cols], local_sems.at[0]),
        pltpu.make_async_copy(probe_hbm, probes.at[0], local_sems.at[1]),
        pltpu.make_async_copy(obj_hbm, obj, local_sems.at[2]),
        pltpu.make_async_copy(meas_hbm.at[0, 0, slot, k_rows], meas, local_sems.at[3]),
    ]
    for load in loads:
        load.start()
    row_at, col_at = pos_ref[0, 0, slot, 0], pos_ref[0, 0, slot, 1]
    live = jnp.where(slot < count_ref[0, 0], 1.0, 0.0).astype(F32)
    columns[0] = jnp.full((8, 128), col_at.astype(F32))
    for load in loads:
        load.wait()
    pl.semaphore_wait(barrier, len(line) + len(plane))

    ma_next, ma_prev = {"ma": lax.rem(ma + 1, n_ma)}, {"ma": lax.rem(ma + n_ma - 1, n_ma)}
    partner = {"gx": gx + 1 - 2 * core}
    ring = {}
    for part, other in ((0, 1), (1, 0)):
        ring["n", part] = copies.make(probes.at[0, core, part], probes.at[1, core, part], ma_next)
        ring["p", other] = copies.make(probes.at[0, core, other], probes.at[3, core, other], ma_prev)
        ring["n", part].start()
        ring["p", other].start()

    above = copies.make(columns.at[0], columns.at[2], {"gx": gx - 1}, up)
    below = copies.make(columns.at[0], columns.at[1], {"gx": gx + 1}, down)
    when(up, above.start)
    when(down, below.start)

    def exchange(condition_low, condition_high, axis, me, low, high):
        first = copies.make(*low, {axis: me - 1}, condition_low)
        second = copies.make(*high, {axis: me + 1}, condition_high)
        when(condition_low, first.start)
        when(condition_high, second.start)
        return ((condition_high, first), (condition_low, second))

    def arrive(arrivals):
        for condition, copy in arrivals:
            when(condition, copy.wait_recv)

    def beside(buf, p, at, rows):
        strip = buf.at[p, pl.ds(at, rows)]
        return exchange(
            left,
            right,
            "gy",
            gy,
            (strip.at[:, pl.ds(rim, rim)], strip.at[:, pl.ds(rim + ty, rim)]),
            (strip.at[:, pl.ds(ty, rim)], strip.at[:, pl.ds(0, rim)]),
        )

    first_beside = [beside(wide.at[0], p, 0, tx) for p in range(2)]

    w_re, w_im = w_ref[0], w_ref[1]
    t_two[:n, :n], t_two[:n, n:], t_two[n:, :n], t_two[n:, n:] = w_re, w_im, -w_im, w_re
    t_back[:n, :n], t_back[:n, n:], t_back[n:, :n], t_back[n:, n:] = w_re, -w_im, w_im, w_re
    wk_re, wk_im = w_ref[0, k_rows, :], w_ref[1, k_rows, :]
    t_one[:kh, :n], t_one[:kh, n:], t_one[kh:, :n], t_one[kh:, n:] = wk_re, -wk_im, wk_im, wk_re
    k_cols = pl.ds(pl.multiple_of(part_k * kh, kh), kh)
    wc_re, wc_im = w_ref[0, :, k_cols], w_ref[1, :, k_cols]
    t_three[:n, :kh], t_three[:n, kh:] = wc_re, wc_im
    t_three[n:, :kh], t_three[n:, kh:] = -wc_im, wc_re

    def clear(ref):
        ref[...] = jnp.zeros(ref.shape, ref.dtype)

    for it in range(OUTER + 1):
        for p in range(2):
            when(gx == 0, functools.partial(clear, cut.at[it, p, pl.ds(0, rim)]))
            when(gx == n_gx - 1, functools.partial(clear, cut.at[it, p, pl.ds(rim + tx, rim)]))
            when(gy == 0, functools.partial(clear, wide.at[it, p, :, pl.ds(0, rim)]))
            when(gy == n_gy - 1, functools.partial(clear, wide.at[it, p, :, pl.ds(rim + ty, rim)]))
            if it < OUTER:
                when(gx == n_gx - 1, functools.partial(clear, from_z.at[it, 0, p]))
                when(gx == 0, functools.partial(clear, from_z.at[it, 1, p]))
                when(gy == n_gy - 1, functools.partial(clear, from_y.at[it, 0, p]))
                when(gy == 0, functools.partial(clear, from_y.at[it, 1, p]))
    when(gx == 0, functools.partial(clear, columns.at[1]))
    when(gx == n_gx - 1, functools.partial(clear, columns.at[2]))

    height, width = 2 * rim + tx, 2 * rim + ty

    def chosen(shape, dim, first):
        here = lax.broadcasted_iota(jnp.int32, shape, dim)
        there = lax.broadcasted_iota(jnp.int32, shape, 1 - dim)
        return jnp.where((here - there).astype(F32) == first, 1.0, 0.0).astype(BF16)

    row_first = jnp.full((1, 1), row_at.astype(F32))
    for i in range(2):
        cut_rows[:, i * height : (i + 1) * height] = chosen((n, height), 1, row_first)
        put_rows[:, i * n : (i + 1) * n] = chosen((height, n), 0, row_first)
    arrive(((down, above), (up, below)))
    for which in range(3):
        first = columns[which][:1, :1]
        for i in range(2):
            cut_cols[i * width : (i + 1) * width, which * n : (which + 1) * n] = chosen(
                (width, n), 0, first
            )
            at = (2 * which + i) * n
            put_cols[at : at + n] = chosen((n, width), 1, first)

    def two_terms(x, ref, at, axis):
        top = x.astype(BF16)
        rest = (x - top.astype(F32)).astype(BF16)
        size = x.shape[axis]
        if axis == 0:
            ref[at : at + size], ref[at + size : at + 2 * size] = top, rest
        else:
            ref[:, at : at + size], ref[:, at + size : at + 2 * size] = top, rest

    def dot(x, y):
        return jnp.dot(x, y, preferred_element_type=F32)

    def cut_and_lend(it, p, at):
        rows = pl.ds(at, row_chunk)
        two_terms(wide[it, p, rows], terms_cols, 0, 1)
        x = dot(terms_cols[...], cut_cols[...])
        cut[it, p, pl.ds(rim + at, row_chunk)] = x[:, :n]
        lent[it, 0, p, rows] = x[:, n : 2 * n]
        lent[it, 1, p, rows] = x[:, 2 * n :]
        return exchange(
            up,
            down,
            "gx",
            gx,
            (lent.at[it, 0, p, rows], cut.at[it, p, pl.ds(rim + tx + at, row_chunk)]),
            (lent.at[it, 1, p, rows], cut.at[it, p, pl.ds(at, row_chunk)]),
        )

    def window(it):
        def part(p, _):
            two_terms(cut[it, p], terms_rows, 0, 0)
            win[p] = dot(cut_rows[...], terms_rows[...])
            return 0

        lax.fori_loop(0, 2, part, 0)

    for p in range(2):
        arrive(first_beside[p])
    stacked = [cut_and_lend(0, p, at) for p, at in chunks]
    for arrivals in stacked:
        arrive(arrivals)

    def forward_pair(d):
        for c in range(2):
            pr, pi = probes[d, c, 0], probes[d, c, 1]
            wr, wi = win[0], win[1]
            wave[c, :n] = (pr * wr - pi * wi).astype(BF16)
            wave[c, n:] = (pr * wi + pi * wr).astype(BF16)
            h = dot(t_one[...], wave[c]).astype(BF16)
            half[c * kh : (c + 1) * kh, :n] = h[:kh]
            half[c * kh : (c + 1) * kh, n:] = h[kh:]
        return dot(half[...], t_two[...])

    def pair_rows(d):
        return pl.ds(pl.multiple_of(d * n, n), n)

    def folded(x):
        x = x[:kh] + x[kh:]
        return x[:, :n] + x[:, n:]

    def backward(misfit):
        weight[:, :n] = 2.0 * misfit
        weight[:, n:] = 2.0 * misfit

        def pair(d, _):
            y = weight[...]
            f = spec[pair_rows(d), :]
            half[:kh] = (f[:kh] * y).astype(BF16)
            half[kh:] = (f[kh:] * y).astype(BF16)
            b = dot(half[...], t_back[...]).astype(BF16)
            for c in range(2):
                turned[c, :kh] = b[c * kh : (c + 1) * kh, :n]
                turned[c, kh:] = b[c * kh : (c + 1) * kh, n:]
                g = dot(t_three[...], turned[c])
                pr, pi = probes[d, c, 0], probes[d, c, 1]
                patch[0] += pr * g[:n] + pi * g[n:]
                patch[1] += pr * g[n:] - pi * g[:n]
            return 0

        clear(patch)
        lax.fori_loop(0, n_ma, pair, 0)

    def place(it):
        def part(p, _):
            two_terms(patch[p], terms_patch, 0, 0)
            tall[it, p] = dot(put_rows[...], terms_patch[...])
            return 0

        lax.fori_loop(0, 2, part, 0)

    def combine(it):
        place(it)
        folds = []
        for p, at in chunks:
            rows = pl.ds(at, row_chunk)
            folds.append(
                exchange(
                    up,
                    down,
                    "gx",
                    gx,
                    (tall.at[it, p, rows], from_z.at[it, 0, p, rows]),
                    (tall.at[it, p, pl.ds(rim + tx + at, row_chunk)], from_z.at[it, 1, p, rows]),
                )
            )
        sides = []
        for i, (p, at) in enumerate(chunks):
            rows = pl.ds(at, row_chunk)
            arrive(folds[i])
            two_terms(tall[it, p, pl.ds(rim + at, row_chunk)], terms_put, 0, 1)
            two_terms(from_z[it, 1, p, rows], terms_put, 2 * n, 1)
            two_terms(from_z[it, 0, p, rows], terms_put, 4 * n, 1)
            ext[it, p, rows] = dot(terms_put[...], put_cols[...])
            strip = ext.at[it, p, rows]
            sides.append(
                exchange(
                    left,
                    right,
                    "gy",
                    gy,
                    (strip.at[:, pl.ds(0, rim)], from_y.at[it, 0, p, rows]),
                    (strip.at[:, pl.ds(rim + ty, rim)], from_y.at[it, 1, p, rows]),
                )
            )
        share = row_chunk // n_ma
        parts = []
        for i, (p, at) in enumerate(chunks):
            rows = pl.ds(at, row_chunk)
            arrive(sides[i])
            ext[it, p, rows, pl.ds(ty, rim)] += from_y[it, 0, p, rows]
            ext[it, p, rows, pl.ds(rim, rim)] += from_y[it, 1, p, rows]
            batch = []
            for o in range(1, n_ma):
                peer = lax.rem(ma + o, n_ma)
                theirs = pl.ds(pl.multiple_of(at + peer * share, share), share)
                copy = copies.make(
                    ext.at[it, p, theirs, own_cols], from_ma.at[it, o - 1, i], {"ma": peer}
                )
                copy.start()
                batch.append(copy)
            parts.append(batch)
        gathers, square = [], jnp.zeros((8, 128), F32)
        for i, (p, at) in enumerate(chunks):
            mine = pl.ds(pl.multiple_of(at + ma * share, share), share)
            total = ext[it, p, mine, own_cols]
            for o in range(1, n_ma):
                parts[i][o - 1].wait_recv()
                total += from_ma[it, o - 1, i]
            wide[it + 1, p, mine, own_cols] = -total
            square += squares(total)
            batch = []
            for o in range(1, n_ma):
                ours = wide.at[it + 1, p, mine, own_cols]
                copy = copies.make(ours, ours, {"ma": lax.rem(ma + o, n_ma)})
                copy.start()
                batch.append(copy)
            gathers.append(batch)
        sides = []
        for i, (p, at) in enumerate(chunks):
            for copy in gathers[i]:
                copy.wait_recv()
            sides.append(beside(wide.at[it + 1], p, at, row_chunk))
        stacked = []
        for i, (p, at) in enumerate(chunks):
            arrive(sides[i])
            stacked.append(cut_and_lend(it + 1, p, at))
        for arrivals in stacked:
            arrive(arrivals)
        return square

    def squares(x):
        x = x * x
        out = x[:, :128]
        for i in range(1, x.shape[1] // 128):
            out = out + x[:, i * 128 : (i + 1) * 128]
        return jnp.sum(out.reshape(-1, 8, 128), axis=0)

    def row_of(x):
        x = jnp.sum(x, axis=0, keepdims=True)
        return x + pltpu.roll(x, 64, 1)

    def step_size(it, square, changes):
        lane = lax.broadcasted_iota(jnp.int32, (1, 128), 1)
        value = jnp.where(lane < 64, row_of(square), row_of(changes))
        for buf, me, devices in (
            (sums_plane, gy * n_ma + ma, plane),
            (sums_line, gx, line),
        ):
            buf[it, me] = value
            batch = []
            for device in devices:
                mine = buf.at[it, me]
                copy = copies.make(mine, mine, device)
                copy.start()
                batch.append(copy)
            for copy in batch:
                copy.wait_recv()
            value = buf[it, 0]
            for i in range(1, len(devices) + 1):
                value += buf[it, i]
        norm = jnp.sum(jnp.where(lane < 64, value, 0.0), keepdims=True)
        change = jnp.sum(jnp.where(lane < 64, 0.0, value), keepdims=True)
        return norm / (change + DAMPING * norm)

    window(0)
    intensity = jnp.zeros((kh, n), F32)

    def hand(d, part):
        copy = copies.make(probes.at[d, core, part], probes.at[d, core, part], partner)
        copy.start()
        return copy

    handed = {}
    for part, other in ((0, 1), (1, 0)):
        ring["n", part].wait_recv()
        ring["p", other].wait_recv()
        if part == 0:
            forth = copies.make(probes.at[1, core, 0], probes.at[2, core, 0], ma_next)
            back = copies.make(probes.at[3, core, 1], probes.at[2, core, 1], ma_prev)
            forth.start()
            back.start()
        handed[1, part] = hand(1, part)
        handed[3, other] = hand(3, other)
        if part == 0:
            f = forward_pair(0)
            spec[pair_rows(0), :] = f
            intensity += folded(f * f)
    for d in (1, 3):
        handed[d, 0].wait_recv()
        handed[d, 1].wait_recv()
        f = forward_pair(d)
        spec[pair_rows(d), :] = f
        intensity += folded(f * f)
    forth.wait_recv()
    handed[2, 0] = hand(2, 0)
    back.wait_recv()
    handed[2, 1] = hand(2, 1)
    handed[2, 0].wait_recv()
    handed[2, 1].wait_recv()
    f = forward_pair(2)
    spec[pair_rows(2), :] = f
    intensity += folded(f * f)

    for it in range(OUTER):
        backward(live * (intensity - meas[...]))
        square = combine(it)
        window(it + 1)
        last = it + 1 == OUTER

        def pair(d, change, last=last):
            m = forward_pair(d)
            if not last:
                moved[pair_rows(d), :] = m
            return change + folded(spec[pair_rows(d), :] * m)

        change = live * 2.0 * lax.fori_loop(0, n_ma, pair, jnp.zeros((kh, n), F32))
        alpha = step_size(it, square, squares(change))
        obj[...] += alpha * wide[it + 1, :, :, own_cols]
        if not last:

            def advance(d, total, alpha=alpha):
                f = spec[pair_rows(d), :] + alpha * moved[pair_rows(d), :]
                spec[pair_rows(d), :] = f
                return total + folded(f * f)

            intensity = lax.fori_loop(0, n_ma, advance, jnp.zeros((kh, n), F32))
    out_ref[...] = obj[...]
    copies.finish()


def solution(mesh):
    sizes = (mesh.shape["gx"], mesh.shape["gy"], mesh.shape["ma"])

    def shards(object_field, probe_modes, measured, positions, slot_counts):
        n = probe_modes.shape[-1]
        _, tx, ty = object_field.shape
        rim, kh = n // 2, n // 2
        height, width = tx + 2 * rim, ty + 2 * rim
        modes = probe_modes.shape[0] * sizes[2]
        row_chunk = tx // 2
        vmem = pltpu.VMEM
        scratch = [
            vmem((2, tx, ty), F32),
            vmem((OUTER + 1, 2, tx, width), F32),
            vmem((OUTER + 1, 2, height, n), F32),
            vmem((OUTER + 1, 2, 2, tx, n), F32),
            vmem((sizes[2], 2, 2, n, n), F32),
            vmem((kh, n), F32),
            vmem((n, 2 * n), BF16),
            vmem((2 * n, 2 * n), BF16),
            vmem((2 * n, 2 * n), BF16),
            vmem((2 * n, n), BF16),
            vmem((2, n, n), F32),
            vmem((2, 2 * n, n), BF16),
            vmem((n, 2 * n), BF16),
            vmem((modes * kh, 2 * n), F32),
            vmem((modes * kh, 2 * n), F32),
            vmem((2, n, n), BF16),
            vmem((kh, 2 * n), F32),
            vmem((2, n, n), F32),
            vmem((OUTER, 2, height, n), F32),
            vmem((n, 2 * height), BF16),
            vmem((2 * width, 3 * n), BF16),
            vmem((height, 2 * n), BF16),
            vmem((6 * n, width), BF16),
            vmem((3, 8, 128), F32),
            vmem((row_chunk, 2 * width), BF16),
            vmem((2 * height, n), BF16),
            vmem((2 * n, n), BF16),
            vmem((row_chunk, 6 * n), BF16),
            vmem((OUTER, 2, tx, width), F32),
            vmem((OUTER, 2, 2, tx, n), F32),
            vmem((OUTER, 2, 2, tx, rim), F32),
            vmem((OUTER, sizes[2] - 1, 4, row_chunk // sizes[2], ty), F32),
            vmem((OUTER, sizes[1] * sizes[2], 1, 128), F32),
            vmem((OUTER, sizes[0], 1, 128), F32),
            pltpu.SemaphoreType.DMA((4,)),
            pltpu.SemaphoreType.DMA((208,)),
            pltpu.SemaphoreType.DMA((208,)),
        ]
        anywhere = pl.BlockSpec(memory_space=pl.ANY)
        smem = pl.BlockSpec(memory_space=pltpu.SMEM)
        in_vmem = pl.BlockSpec(memory_space=pltpu.VMEM)
        return pl.pallas_call(
            functools.partial(kernel, (*sizes, n, tx, ty)),
            out_shape=jax.ShapeDtypeStruct(object_field.shape, F32),
            in_specs=[anywhere, anywhere, anywhere, smem, smem, in_vmem],
            out_specs=in_vmem,
            scratch_shapes=scratch,
            compiler_params=pltpu.CompilerParams(
                collective_id=0, has_side_effects=True, vmem_limit_bytes=60 * 1024 * 1024
            ),
        )(object_field, probe_modes, measured, positions, slot_counts, jnp.asarray(dft_parts(n)))

    placed = (
        P(None, "gx", "gy"),
        P("ma", None, None, None),
        P("gx", "gy", None, None, None),
        P("gx", "gy", None, None),
        P("gx", "gy"),
    )
    return jax.shard_map(
        shards, mesh=mesh, in_specs=placed, out_specs=P(None, "gx", "gy"), check_vma=False
    )
```

time: 135 us -> 115 us (0.85)
  Pallas kernels: 132 us -> 112 us
    pallas_call x1, Pallas kernels: 132 us -> 112 us  [shards(): pl.pallas_call(functools.partial(kernel, (*sizes, n, tx, ty)), out_shape=...]
where the time goes in v3:
time: 115 us
  Pallas kernels  112 us (97%)
  local copies, waits for them, and re-layouts  1.67 us (1%)
    pallas_call x1, Pallas kernels, shards(): pl.pallas_call(functools.partial(kernel, (*sizes, n, tx, ty)), out_shape=...  112 us

profile of v3, /device:TPU:1, one launch (start us, length us, event | category | flops | bytes accessed | tf_op | source)
XLA Modules:
  0.0 114.7 jit_solution(5740317766144616869)
XLA Ops:
  0.7 112.3 %shard_map.64 = f32[2,128,256]{2,1,0:T(8,128)} custom-call(f32[2,128,256]{2,1,0:T(8,128)} %obj_hbm.1, f32[2,2,256,256]{3,2,1,0:T(8,128)} %probe_hbm.1, f32[1,1,2,256,256]{4,3,2,1,0:T(8,128)} %meas_hbm.1, s32[1,1,2,2]{3,2,1,0:T(2,128)} %pos_ref.1, s32[1,1]{1,0:T(1,128)S(6)} %copy.8.count_ref, bf16[2,256,256]{2,1,0:T(8,128)(2,1)} %constant.2.clone.w_ref), custom_call_target="tpu_custom_call" | custom-call | tf_op jit(solution)/shard_map/pallas_call | solution.py:551
  113.0 1.7 %copy.9 = f32[2,128,256]{2,1,0:T(8,128)} copy(f32[2,128,256]{2,1,0:T(8,128)} %shard_map.64) | data formatting | bytes 524288

commit v4 on v3

--- a/solution.py
+++ b/solution.py
@@ -97,6 +97,7 @@
     from_ma,
     sums_plane,
     sums_line,
+    token,
     local_sems,
     send_sems,
     recv_sems,
@@ -119,8 +120,18 @@
         {"gy": lax.rem(gy + o // n_ma, n_gy), "ma": lax.rem(ma + o % n_ma, n_ma)}
         for o in range(1, n_gy * n_ma)
     ]
-    for device in line + plane:
-        pl.semaphore_signal(barrier, inc=1, device_id=device, device_id_type=MESH)
+
+    def at_distance(axis, o):
+        me, size = {"gx": (gx, n_gx), "gy": (gy, n_gy), "ma": (ma, n_ma)}[axis]
+        offsets = {o % size, (size - o) % size}
+        return [{axis: lax.rem(me + off, size)} for off in sorted(offsets)]
+
+    def tell(sem, devices):
+        for device in devices:
+            pl.semaphore_signal(sem, inc=1, device_id=device, device_id_type=MESH)
+
+    nearest = at_distance("gx", 1) + at_distance("gy", 1) + at_distance("ma", 1)
+    tell(barrier, nearest)
 
     k_rows = pl.ds(pl.multiple_of(part_k * kh, kh), kh)
     own_cols = pl.ds(rim, ty)
@@ -135,48 +146,6 @@
     row_at, col_at = pos_ref[0, 0, slot, 0], pos_ref[0, 0, slot, 1]
     live = jnp.where(slot < count_ref[0, 0], 1.0, 0.0).astype(F32)
     columns[0] = jnp.full((8, 128), col_at.astype(F32))
-    for load in loads:
-        load.wait()
-    pl.semaphore_wait(barrier, len(line) + len(plane))
-
-    ma_next, ma_prev = {"ma": lax.rem(ma + 1, n_ma)}, {"ma": lax.rem(ma + n_ma - 1, n_ma)}
-    partner = {"gx": gx + 1 - 2 * core}
-    ring = {}
-    for part, other in ((0, 1), (1, 0)):
-        ring["n", part] = copies.make(probes.at[0, core, part], probes.at[1, core, part], ma_next)
-        ring["p", other] = copies.make(probes.at[0, core, other], probes.at[3, core, other], ma_prev)
-        ring["n", part].start()
-        ring["p", other].start()
-
-    above = copies.make(columns.at[0], columns.at[2], {"gx": gx - 1}, up)
-    below = copies.make(columns.at[0], columns.at[1], {"gx": gx + 1}, down)
-    when(up, above.start)
-    when(down, below.start)
-
-    def exchange(condition_low, condition_high, axis, me, low, high):
-        first = copies.make(*low, {axis: me - 1}, condition_low)
-        second = copies.make(*high, {axis: me + 1}, condition_high)
-        when(condition_low, first.start)
-        when(condition_high, second.start)
-        return ((condition_high, first), (condition_low, second))
-
-    def arrive(arrivals):
-        for condition, copy in arrivals:
-            when(condition, copy.wait_recv)
-
-    def beside(buf, p, at, rows):
-        strip = buf.at[p, pl.ds(at, rows)]
-        return exchange(
-            left,
-            right,
-            "gy",
-            gy,
-            (strip.at[:, pl.ds(rim, rim)], strip.at[:, pl.ds(rim + ty, rim)]),
-            (strip.at[:, pl.ds(ty, rim)], strip.at[:, pl.ds(0, rim)]),
-        )
-
-    first_beside = [beside(wide.at[0], p, 0, tx) for p in range(2)]
-
     w_re, w_im = w_ref[0], w_ref[1]
     t_two[:n, :n], t_two[:n, n:], t_two[n:, :n], t_two[n:, n:] = w_re, w_im, -w_im, w_re
     t_back[:n, :n], t_back[:n, n:], t_back[n:, :n], t_back[n:, n:] = w_re, -w_im, w_im, w_re
@@ -215,15 +184,77 @@
     for i in range(2):
         cut_rows[:, i * height : (i + 1) * height] = chosen((n, height), 1, row_first)
         put_rows[:, i * n : (i + 1) * n] = chosen((height, n), 0, row_first)
-    arrive(((down, above), (up, below)))
-    for which in range(3):
+
+    def set_columns(which):
         first = columns[which][:1, :1]
-        for i in range(2):
-            cut_cols[i * width : (i + 1) * width, which * n : (which + 1) * n] = chosen(
-                (width, n), 0, first
-            )
-            at = (2 * which + i) * n
-            put_cols[at : at + n] = chosen((n, width), 1, first)
+        cut_cols[:, which * n : (which + 1) * n] = chosen((width, n), 0, first)
+        put_cols[which * n : (which + 1) * n] = chosen((n, width), 1, first)
+
+    set_columns(0)
+
+    for load in loads:
+        load.wait()
+    pl.semaphore_wait(barrier, len(nearest))
+
+    ma_next, ma_prev = {"ma": lax.rem(ma + 1, n_ma)}, {"ma": lax.rem(ma + n_ma - 1, n_ma)}
+    gy_next, gy_prev = {"gy": lax.rem(gy + 1, n_gy)}, {"gy": lax.rem(gy + n_gy - 1, n_gy)}
+    partner = {"gx": gx + 1 - 2 * core}
+    mine_part = lax.rem(gy, 2)
+    halves = (pl.ds(0, kh), pl.ds(kh, kh))
+
+    def piece(d, part, h):
+        return probes.at[d, core, part, halves[h]]
+
+    def send(src, dst, device):
+        copy = copies.make(src, dst, device)
+        copy.start()
+        return copy
+
+    ring = {}
+    for h, g in ((0, 1), (1, 0)):
+        ring[1, h] = send(piece(0, mine_part, h), piece(1, mine_part, h), ma_next)
+        ring[3, g] = send(piece(0, mine_part, g), piece(3, mine_part, g), ma_prev)
+
+    above = copies.make(columns.at[0], columns.at[2], {"gx": gx - 1}, up)
+    below = copies.make(columns.at[0], columns.at[1], {"gx": gx + 1}, down)
+    when(up, above.start)
+    when(down, below.start)
+
+    def exchange(condition_low, condition_high, axis, me, low, high):
+        first = copies.make(*low, {axis: me - 1}, condition_low)
+        second = copies.make(*high, {axis: me + 1}, condition_high)
+        when(condition_low, first.start)
+        when(condition_high, second.start)
+        return ((condition_high, first), (condition_low, second))
+
+    def arrive(arrivals):
+        for condition, copy in arrivals:
+            when(condition, copy.wait_recv)
+
+    def beside(buf, p, at, rows):
+        strip = buf.at[p, pl.ds(at, rows)]
+        return exchange(
+            left,
+            right,
+            "gy",
+            gy,
+            (strip.at[:, pl.ds(rim, rim)], strip.at[:, pl.ds(rim + ty, rim)]),
+            (strip.at[:, pl.ds(ty, rim)], strip.at[:, pl.ds(0, rim)]),
+        )
+
+    first_beside = [beside(wide.at[0], p, 0, tx) for p in range(2)]
+
+    tell(token.at[0], at_distance("gx", 1))
+    tell(token.at[3], at_distance("gy", 1) + at_distance("ma", 1))
+    pl.semaphore_wait(token.at[0], 2)
+    tell(token.at[1], at_distance("gx", 2))
+    pl.semaphore_wait(token.at[3], 4)
+    tell(token.at[4], at_distance("gy", 2) + at_distance("ma", 2))
+    pl.semaphore_wait(token.at[1], 2)
+    tell(token.at[2], at_distance("gx", 4))
+    pl.semaphore_wait(token.at[4], 2)
+    pl.semaphore_wait(token.at[2], 2)
+
 
     def two_terms(x, ref, at, axis):
         top = x.astype(BF16)
@@ -237,10 +268,20 @@
     def dot(x, y):
         return jnp.dot(x, y, preferred_element_type=F32)
 
+    def stack(x, ref, at):
+        rows, cols = x.shape
+        top = x.astype(BF16)
+        ref[:rows, at : at + cols] = top
+        ref[rows:, at : at + cols] = (x - top.astype(F32)).astype(BF16)
+
+    def both(x):
+        rows = x.shape[0] // 2
+        return x[:rows] + x[rows:]
+
     def cut_and_lend(it, p, at):
         rows = pl.ds(at, row_chunk)
-        two_terms(wide[it, p, rows], terms_cols, 0, 1)
-        x = dot(terms_cols[...], cut_cols[...])
+        stack(wide[it, p, rows], terms_cols, 0)
+        x = both(dot(terms_cols[...], cut_cols[...]))
         cut[it, p, pl.ds(rim + at, row_chunk)] = x[:, :n]
         lent[it, 0, p, rows] = x[:, n : 2 * n]
         lent[it, 1, p, rows] = x[:, 2 * n :]
@@ -261,12 +302,6 @@
 
         lax.fori_loop(0, 2, part, 0)
 
-    for p in range(2):
-        arrive(first_beside[p])
-    stacked = [cut_and_lend(0, p, at) for p, at in chunks]
-    for arrivals in stacked:
-        arrive(arrivals)
-
     def forward_pair(d):
         for c in range(2):
             pr, pi = probes[d, c, 0], probes[d, c, 1]
@@ -285,13 +320,16 @@
         x = x[:kh] + x[kh:]
         return x[:, :n] + x[:, n:]
 
-    def backward(misfit):
+    def backward(misfit, alpha):
         weight[:, :n] = 2.0 * misfit
         weight[:, n:] = 2.0 * misfit
 
         def pair(d, _):
             y = weight[...]
             f = spec[pair_rows(d), :]
+            if alpha is not None:
+                f = f + alpha * moved[pair_rows(d), :]
+                spec[pair_rows(d), :] = f
             half[:kh] = (f[:kh] * y).astype(BF16)
             half[kh:] = (f[kh:] * y).astype(BF16)
             b = dot(half[...], t_back[...]).astype(BF16)
@@ -305,7 +343,7 @@
             return 0
 
         clear(patch)
-        lax.fori_loop(0, n_ma, pair, 0)
+        lax.fori_loop(0, n_ma, pair, 0, unroll=True)
 
     def place(it):
         def part(p, _):
@@ -334,10 +372,10 @@
         for i, (p, at) in enumerate(chunks):
             rows = pl.ds(at, row_chunk)
             arrive(folds[i])
-            two_terms(tall[it, p, pl.ds(rim + at, row_chunk)], terms_put, 0, 1)
-            two_terms(from_z[it, 1, p, rows], terms_put, 2 * n, 1)
-            two_terms(from_z[it, 0, p, rows], terms_put, 4 * n, 1)
-            ext[it, p, rows] = dot(terms_put[...], put_cols[...])
+            stack(tall[it, p, pl.ds(rim + at, row_chunk)], terms_put, 0)
+            stack(from_z[it, 1, p, rows], terms_put, n)
+            stack(from_z[it, 0, p, rows], terms_put, 2 * n)
+            ext[it, p, rows] = both(dot(terms_put[...], put_cols[...]))
             strip = ext.at[it, p, rows]
             sides.append(
                 exchange(
@@ -414,12 +452,10 @@
             (sums_line, gx, line),
         ):
             buf[it, me] = value
-            batch = []
-            for device in devices:
-                mine = buf.at[it, me]
-                copy = copies.make(mine, mine, device)
-                copy.start()
-                batch.append(copy)
+            mine = buf.at[it, me]
+            batch = [send(mine, mine, device) for device in devices]
+            if devices is plane:
+                yield
             for copy in batch:
                 copy.wait_recv()
             value = buf[it, 0]
@@ -427,49 +463,72 @@
                 value += buf[it, i]
         norm = jnp.sum(jnp.where(lane < 64, value, 0.0), keepdims=True)
         change = jnp.sum(jnp.where(lane < 64, 0.0, value), keepdims=True)
-        return norm / (change + DAMPING * norm)
-
-    window(0)
+        yield norm / (change + DAMPING * norm)
+
     intensity = jnp.zeros((kh, n), F32)
 
-    def hand(d, part):
-        copy = copies.make(probes.at[d, core, part], probes.at[d, core, part], partner)
-        copy.start()
-        return copy
-
-    handed = {}
-    for part, other in ((0, 1), (1, 0)):
-        ring["n", part].wait_recv()
-        ring["p", other].wait_recv()
-        if part == 0:
-            forth = copies.make(probes.at[1, core, 0], probes.at[2, core, 0], ma_next)
-            back = copies.make(probes.at[3, core, 1], probes.at[2, core, 1], ma_prev)
-            forth.start()
-            back.start()
-        handed[1, part] = hand(1, part)
-        handed[3, other] = hand(3, other)
-        if part == 0:
-            f = forward_pair(0)
-            spec[pair_rows(0), :] = f
-            intensity += folded(f * f)
-    for d in (1, 3):
-        handed[d, 0].wait_recv()
-        handed[d, 1].wait_recv()
+    def add_spectra(d, total):
         f = forward_pair(d)
         spec[pair_rows(d), :] = f
-        intensity += folded(f * f)
-    forth.wait_recv()
-    handed[2, 0] = hand(2, 0)
-    back.wait_recv()
-    handed[2, 1] = hand(2, 1)
-    handed[2, 0].wait_recv()
-    handed[2, 1].wait_recv()
-    f = forward_pair(2)
-    spec[pair_rows(2), :] = f
-    intensity += folded(f * f)
-
+        return total + folded(f * f)
+
+    other_part = 1 - mine_part
+    passed, handed = {}, {}
+
+    def pass_on(d, h):
+        ours = piece(d, mine_part, h)
+        passed[d, h] = send(ours, ours, gy_prev if h else gy_next)
+        handed[d, h] = send(ours, ours, partner)
+
+    def hand_on(d, h):
+        theirs = piece(d, other_part, h)
+        passed[d, h].wait_recv()
+        handed[d, h, 1] = send(theirs, theirs, partner)
+
+    def complete(d):
+        for h in range(2):
+            handed[d, h].wait_recv()
+            handed[d, h, 1].wait_recv()
+
+    arrive(((down, above), (up, below)))
+    set_columns(1)
+    set_columns(2)
+    ring[1, 0].wait_recv()
+    ring[2, 0] = send(piece(1, mine_part, 0), piece(2, mine_part, 0), ma_next)
+    pass_on(1, 0)
+    ring[3, 1].wait_recv()
+    ring[2, 1] = send(piece(3, mine_part, 1), piece(2, mine_part, 1), ma_prev)
+    pass_on(3, 1)
+    for p in range(2):
+        arrive(first_beside[p])
+    stacked = [cut_and_lend(0, p, at) for p, at in chunks]
+    ring[1, 1].wait_recv()
+    pass_on(1, 1)
+    ring[3, 0].wait_recv()
+    pass_on(3, 0)
+    for arrivals in stacked:
+        arrive(arrivals)
+    window(0)
+    hand_on(1, 0)
+    hand_on(3, 1)
+    intensity = add_spectra(0, intensity)
+    ring[2, 0].wait_recv()
+    pass_on(2, 0)
+    ring[2, 1].wait_recv()
+    pass_on(2, 1)
+    hand_on(1, 1)
+    hand_on(3, 0)
+    for d in (1, 3):
+        complete(d)
+        intensity = add_spectra(d, intensity)
+    hand_on(2, 0)
+    hand_on(2, 1)
+    complete(2)
+    intensity = add_spectra(2, intensity)
+
+    alpha = None
     for it in range(OUTER):
-        backward(live * (intensity - meas[...]))
+        backward(live * (intensity - meas[...]), alpha)
         square = combine(it)
         window(it + 1)
         last = it + 1 == OUTER
@@ -480,17 +539,20 @@
                 moved[pair_rows(d), :] = m
             return change + folded(spec[pair_rows(d), :] * m)
 
-        change = live * 2.0 * lax.fori_loop(0, n_ma, pair, jnp.zeros((kh, n), F32))
-        alpha = step_size(it, square, squares(change))
+        change = 2.0 * lax.fori_loop(0, n_ma, pair, jnp.zeros((kh, n), F32), unroll=True)
+        sums = step_size(it, square, squares(live * change))
+        next(sums)
+        if not last:
+
+            def power(d, total):
+                m = moved[pair_rows(d), :]
+                return total + folded(m * m)
+
+            moved_power = lax.fori_loop(0, n_ma, power, jnp.zeros((kh, n), F32))
+        alpha = next(sums)
         obj[...] += alpha * wide[it + 1, :, :, own_cols]
         if not last:
-
-            def advance(d, total, alpha=alpha):
-                f = spec[pair_rows(d), :] + alpha * moved[pair_rows(d), :]
-                spec[pair_rows(d), :] = f
-                return total + folded(f * f)
-
-            intensity = lax.fori_loop(0, n_ma, advance, jnp.zeros((kh, n), F32))
+            intensity = intensity + alpha * (change + alpha * moved_power)
     out_ref[...] = obj[...]
     copies.finish()
 
@@ -527,23 +589,24 @@
             vmem((2, n, n), F32),
             vmem((OUTER, 2, height, n), F32),
             vmem((n, 2 * height), BF16),
-            vmem((2 * width, 3 * n), BF16),
+            vmem((width, 3 * n), BF16),
             vmem((height, 2 * n), BF16),
-            vmem((6 * n, width), BF16),
+            vmem((3 * n, width), BF16),
             vmem((3, 8, 128), F32),
-            vmem((row_chunk, 2 * width), BF16),
+            vmem((2 * row_chunk, width), BF16),
             vmem((2 * height, n), BF16),
             vmem((2 * n, n), BF16),
-            vmem((row_chunk, 6 * n), BF16),
+            vmem((2 * row_chunk, 3 * n), BF16),
             vmem((OUTER, 2, tx, width), F32),
             vmem((OUTER, 2, 2, tx, n), F32),
             vmem((OUTER, 2, 2, tx, rim), F32),
             vmem((OUTER, sizes[2] - 1, 4, row_chunk // sizes[2], ty), F32),
             vmem((OUTER, sizes[1] * sizes[2], 1, 128), F32),
             vmem((OUTER, sizes[0], 1, 128), F32),
+            pltpu.SemaphoreType.REGULAR((5,)),
             pltpu.SemaphoreType.DMA((4,)),
-            pltpu.SemaphoreType.DMA((208,)),
-            pltpu.SemaphoreType.DMA((208,)),
+            pltpu.SemaphoreType.DMA((224,)),
+            pltpu.SemaphoreType.DMA((224,)),
         ]
         anywhere = pl.BlockSpec(memory_space=pl.ANY)
         smem = pl.BlockSpec(memory_space=pltpu.SMEM)

time: 115 us -> 108 us (0.939)
  Pallas kernels: 112 us -> 105 us
    pallas_call x1, Pallas kernels: 112 us -> 105 us  [shards(): pl.pallas_call(functools.partial(kernel, (*sizes, n, tx, ty)), out_shape=...]
where the time goes in v4:
time: 108 us; the launch traced here: 107 us
  Pallas kernels  105 us (97%)
  local copies, waits for them, and re-layouts  1.67 us (2%)
    pallas_call x1, Pallas kernels, shards(): pl.pallas_call(functools.partial(kernel, (*sizes, n, tx, ty)), out_shape=...  105 us

profile of v4, /device:TPU:1, one launch (start us, length us, event | category | flops | bytes accessed | tf_op | source)
XLA Modules:
  0.0 107.5 jit_solution(7114368104160183172)
XLA Ops:
  0.7 105.1 %shard_map.64 = f32[2,128,256]{2,1,0:T(8,128)} custom-call(f32[2,128,256]{2,1,0:T(8,128)} %obj_hbm.1, f32[2,2,256,256]{3,2,1,0:T(8,128)} %probe_hbm.1, f32[1,1,2,256,256]{4,3,2,1,0:T(8,128)} %meas_hbm.1, s32[1,1,2,2]{3,2,1,0:T(2,128)} %pos_ref.1, s32[1,1]{1,0:T(1,128)S(6)} %copy.8.count_ref, bf16[2,256,256]{2,1,0:T(8,128)(2,1)} %constant.2.clone.w_ref), custom_call_target="tpu_custom_call" | custom-call | tf_op jit(solution)/shard_map/pallas_call | solution.py:614
  105.8 1.7 %copy.9 = f32[2,128,256]{2,1,0:T(8,128)} copy(f32[2,128,256]{2,1,0:T(8,128)} %shard_map.64) | data formatting | bytes 524288

commit v5 on v4

--- a/solution.py
+++ b/solution.py
@@ -11,6 +11,7 @@
 
 OUTER = 2
 DAMPING = 1.0
+CHUNKS = 4
 MESH = pl.DeviceIdType.MESH
 F32 = jnp.float32
 BF16 = jnp.bfloat16
@@ -59,11 +60,13 @@
     obj_hbm,
     probe_hbm,
     meas_hbm,
+    pos_hbm,
+    count_hbm,
+    w_hbm,
+    out_ref,
     pos_ref,
     count_ref,
     w_ref,
-    out_ref,
-    obj,
     wide,
     cut,
     lent,
@@ -111,8 +114,8 @@
     up, down = gx > 0, gx < n_gx - 1
     left, right = gy > 0, gy < n_gy - 1
     copies = Copies(send_sems, recv_sems)
-    row_chunk = tx // 2
-    chunks = [(p, j * row_chunk) for p in range(2) for j in range(2)]
+    row_chunk = tx // CHUNKS
+    chunks = [(p, j * row_chunk) for p in range(2) for j in range(CHUNKS)]
 
     barrier = pltpu.get_barrier_semaphore()
     line = [{"gx": lax.rem(gx + o, n_gx)} for o in range(1, n_gx)]
@@ -135,17 +138,27 @@
 
     k_rows = pl.ds(pl.multiple_of(part_k * kh, kh), kh)
     own_cols = pl.ds(rim, ty)
+    table_load = pltpu.make_async_copy(w_hbm, w_ref, local_sems.at[4])
+    table_load.start()
+    scalar_loads = [
+        pltpu.make_async_copy(pos_hbm, pos_ref, local_sems.at[2]),
+        pltpu.make_async_copy(count_hbm, count_ref, local_sems.at[5]),
+    ]
+    for load in scalar_loads:
+        load.start()
     loads = [
         pltpu.make_async_copy(obj_hbm, wide.at[0, :, :, own_cols], local_sems.at[0]),
         pltpu.make_async_copy(probe_hbm, probes.at[0], local_sems.at[1]),
-        pltpu.make_async_copy(obj_hbm, obj, local_sems.at[2]),
         pltpu.make_async_copy(meas_hbm.at[0, 0, slot, k_rows], meas, local_sems.at[3]),
     ]
     for load in loads:
         load.start()
+    for load in scalar_loads:
+        load.wait()
     row_at, col_at = pos_ref[0, 0, slot, 0], pos_ref[0, 0, slot, 1]
     live = jnp.where(slot < count_ref[0, 0], 1.0, 0.0).astype(F32)
     columns[0] = jnp.full((8, 128), col_at.astype(F32))
+    table_load.wait()
     w_re, w_im = w_ref[0], w_ref[1]
     t_two[:n, :n], t_two[:n, n:], t_two[n:, :n], t_two[n:, n:] = w_re, w_im, -w_im, w_re
     t_back[:n, :n], t_back[:n, n:], t_back[n:, :n], t_back[n:, n:] = w_re, -w_im, w_im, w_re
@@ -506,23 +519,24 @@
     pass_on(1, 1)
     ring[3, 0].wait_recv()
     pass_on(3, 0)
-    for arrivals in stacked:
-        arrive(arrivals)
-    window(0)
     hand_on(1, 0)
     hand_on(3, 1)
-    intensity = add_spectra(0, intensity)
     ring[2, 0].wait_recv()
     pass_on(2, 0)
     ring[2, 1].wait_recv()
     pass_on(2, 1)
+    for arrivals in stacked:
+        arrive(arrivals)
+    window(0)
     hand_on(1, 1)
     hand_on(3, 0)
-    for d in (1, 3):
-        complete(d)
-        intensity = add_spectra(d, intensity)
+    intensity = add_spectra(0, intensity)
+    complete(1)
+    intensity = add_spectra(1, intensity)
     hand_on(2, 0)
     hand_on(2, 1)
+    complete(3)
+    intensity = add_spectra(3, intensity)
     complete(2)
     intensity = add_spectra(2, intensity)
 
@@ -550,10 +564,10 @@
 
             moved_power = lax.fori_loop(0, n_ma, power, jnp.zeros((kh, n), F32))
         alpha = next(sums)
-        obj[...] += alpha * wide[it + 1, :, :, own_cols]
+        step = alpha * wide[it + 1, :, :, own_cols]
+        out_ref[...] = step if it == 0 else out_ref[...] + step
         if not last:
             intensity = intensity + alpha * (change + alpha * moved_power)
-    out_ref[...] = obj[...]
     copies.finish()
 
 
@@ -566,10 +580,12 @@
         rim, kh = n // 2, n // 2
         height, width = tx + 2 * rim, ty + 2 * rim
         modes = probe_modes.shape[0] * sizes[2]
-        row_chunk = tx // 2
+        row_chunk = tx // CHUNKS
         vmem = pltpu.VMEM
         scratch = [
-            vmem((2, tx, ty), F32),
+            pltpu.SMEM(positions.shape, jnp.int32),
+            pltpu.SMEM(slot_counts.shape, jnp.int32),
+            vmem((2, n, n), BF16),
             vmem((OUTER + 1, 2, tx, width), F32),
             vmem((OUTER + 1, 2, height, n), F32),
             vmem((OUTER + 1, 2, 2, tx, n), F32),
@@ -600,27 +616,27 @@
             vmem((OUTER, 2, tx, width), F32),
             vmem((OUTER, 2, 2, tx, n), F32),
             vmem((OUTER, 2, 2, tx, rim), F32),
-            vmem((OUTER, sizes[2] - 1, 4, row_chunk // sizes[2], ty), F32),
+            vmem((OUTER, sizes[2] - 1, 2 * CHUNKS, row_chunk // sizes[2], ty), F32),
             vmem((OUTER, sizes[1] * sizes[2], 1, 128), F32),
             vmem((OUTER, sizes[0], 1, 128), F32),
             pltpu.SemaphoreType.REGULAR((5,)),
-            pltpu.SemaphoreType.DMA((4,)),
-            pltpu.SemaphoreType.DMA((224,)),
-            pltpu.SemaphoreType.DMA((224,)),
+            pltpu.SemaphoreType.DMA((6,)),
+            pltpu.SemaphoreType.DMA((112 + 56 * CHUNKS,)),
+            pltpu.SemaphoreType.DMA((112 + 56 * CHUNKS,)),
         ]
         anywhere = pl.BlockSpec(memory_space=pl.ANY)
-        smem = pl.BlockSpec(memory_space=pltpu.SMEM)
         in_vmem = pl.BlockSpec(memory_space=pltpu.VMEM)
-        return pl.pallas_call(
+        update = pl.pallas_call(
             functools.partial(kernel, (*sizes, n, tx, ty)),
-            out_shape=jax.ShapeDtypeStruct(object_field.shape, F32),
-            in_specs=[anywhere, anywhere, anywhere, smem, smem, in_vmem],
+            out_shape=pltpu.VMEM(object_field.shape, F32),
+            in_specs=[anywhere] * 6,
             out_specs=in_vmem,
             scratch_shapes=scratch,
             compiler_params=pltpu.CompilerParams(
                 collective_id=0, has_side_effects=True, vmem_limit_bytes=60 * 1024 * 1024
             ),
         )(object_field, probe_modes, measured, positions, slot_counts, jnp.asarray(dft_parts(n)))
+        return object_field + update
 
     placed = (
         P(None, "gx", "gy"),

time: 108 us -> 103 us (0.954)
  Pallas kernels: 105 us -> 102 us
  local copies, waits for them, and re-layouts: 1.67 us -> 0.01 us
    pallas_call x1, Pallas kernels: 105 us -> 102 us  [shards(): pl.pallas_call(functools.partial(kernel, (*sizes, n, tx, ty)), out_shape=...]
    unnamed x1 -> x2, local copies, waits for them, and re-layouts: 1.67 us -> 0.01 us
where the time goes in v5:
time: 103 us
  Pallas kernels  102 us (99%)
    pallas_call x1, Pallas kernels, shards(): pl.pallas_call(functools.partial(kernel, (*sizes, n, tx, ty)), out_shape=...  102 us

profile of v5, /device:TPU:1, one launch (start us, length us, event | category | flops | bytes accessed | tf_op | source)
XLA Modules:
  0.0 103.4 jit_solution(12852824810842314241)
XLA Ops:
  0.7 0.0 copy-start
  0.7 101.9 %shard_map.64 = f32[2,128,256]{2,1,0:T(8,128)S(1)} custom-call(f32[2,128,256]{2,1,0:T(8,128)} %obj_hbm.1, f32[2,2,256,256]{3,2,1,0:T(8,128)} %probe_hbm.1, f32[1,1,2,256,256]{4,3,2,1,0:T(8,128)} %meas_hbm.1, s32[1,1,2,2]{3,2,1,0:T(2,128)} %pos_hbm.1, s32[1,1]{1,0:T(1,128)S(6)} %copy.7.count_hbm, bf16[2,256,256]{2,1,0:T(8,128)(2,1)} %constant.2.clone.w_hbm), custom_call_target="tpu_custom_call" | custom-call | tf_op jit(solution)/shard_map/pallas_call | solution.py:629
  102.6 0.0 copy-done
  102.6 0.7 add.3
Async XLA Ops:
  0.7 102.0 %copy-start = (f32[2,128,256]{2,1,0:T(8,128)S(1)}, f32[2,128,256]{2,1,0:T(8,128)}, u32[]{:S(2)}) copy-start(f32[2,128,256]{2,1,0:T(8,128)} %obj_hbm.1) | copy-start | bytes 786436

commit v6 on v5

--- a/solution.py
+++ b/solution.py
@@ -11,6 +11,8 @@
 
 OUTER = 2
 DAMPING = 1.0
+PIECES = 4
+GROUP = 4
 CHUNKS = 4
 MESH = pl.DeviceIdType.MESH
 F32 = jnp.float32
@@ -94,6 +96,7 @@
     terms_rows,
     terms_patch,
     terms_put,
+    terms_own,
     ext,
     from_z,
     from_y,
@@ -213,10 +216,10 @@
     gy_next, gy_prev = {"gy": lax.rem(gy + 1, n_gy)}, {"gy": lax.rem(gy + n_gy - 1, n_gy)}
     partner = {"gx": gx + 1 - 2 * core}
     mine_part = lax.rem(gy, 2)
-    halves = (pl.ds(0, kh), pl.ds(kh, kh))
+    step = n // PIECES
 
     def piece(d, part, h):
-        return probes.at[d, core, part, halves[h]]
+        return probes.at[d, core, part, pl.ds(h * step, step)]
 
     def send(src, dst, device):
         copy = copies.make(src, dst, device)
@@ -224,7 +227,8 @@
         return copy
 
     ring = {}
-    for h, g in ((0, 1), (1, 0)):
+    for h in range(PIECES):
+        g = PIECES - 1 - h
         ring[1, h] = send(piece(0, mine_part, h), piece(1, mine_part, h), ma_next)
         ring[3, g] = send(piece(0, mine_part, g), piece(3, mine_part, g), ma_prev)
 
@@ -291,21 +295,24 @@
         rows = x.shape[0] // 2
         return x[:rows] + x[rows:]
 
-    def cut_and_lend(it, p, at):
-        rows = pl.ds(at, row_chunk)
-        stack(wide[it, p, rows], terms_cols, 0)
-        x = both(dot(terms_cols[...], cut_cols[...]))
-        cut[it, p, pl.ds(rim + at, row_chunk)] = x[:, :n]
-        lent[it, 0, p, rows] = x[:, n : 2 * n]
-        lent[it, 1, p, rows] = x[:, 2 * n :]
+    def lend(it, p, at, count):
+        rows = pl.ds(at, count)
+        stack(wide[it, p, rows], terms_cols.at[: 2 * count], 0)
+        x = both(dot(terms_cols[: 2 * count], cut_cols[:, n:]))
+        lent[it, 0, p, rows] = x[:, :n]
+        lent[it, 1, p, rows] = x[:, n:]
         return exchange(
             up,
             down,
             "gx",
             gx,
-            (lent.at[it, 0, p, rows], cut.at[it, p, pl.ds(rim + tx + at, row_chunk)]),
-            (lent.at[it, 1, p, rows], cut.at[it, p, pl.ds(at, row_chunk)]),
+            (lent.at[it, 0, p, rows], cut.at[it, p, pl.ds(rim + tx + at, count)]),
+            (lent.at[it, 1, p, rows], cut.at[it, p, pl.ds(at, count)]),
         )
+
+    def keep(it, p):
+        stack(wide[it, p], terms_cols, 0)
+        cut[it, p, pl.ds(rim, tx)] = both(dot(terms_cols[...], cut_cols[:, :n]))
 
     def window(it):
         def part(p, _):
@@ -315,48 +322,53 @@
 
         lax.fori_loop(0, 2, part, 0)
 
-    def forward_pair(d):
-        for c in range(2):
-            pr, pi = probes[d, c, 0], probes[d, c, 1]
+    def group_rows(first, count):
+        return pl.ds(pl.multiple_of(first * n, n), count * n)
+
+    def forward(first, count):
+        for c in range(2 * count):
+            d = first + c // 2
+            pr, pi = probes[d, c % 2, 0], probes[d, c % 2, 1]
             wr, wi = win[0], win[1]
             wave[c, :n] = (pr * wr - pi * wi).astype(BF16)
             wave[c, n:] = (pr * wi + pi * wr).astype(BF16)
             h = dot(t_one[...], wave[c]).astype(BF16)
             half[c * kh : (c + 1) * kh, :n] = h[:kh]
             half[c * kh : (c + 1) * kh, n:] = h[kh:]
-        return dot(half[...], t_two[...])
-
-    def pair_rows(d):
-        return pl.ds(pl.multiple_of(d * n, n), n)
+        return dot(half[: count * n], t_two[...])
 
     def folded(x):
-        x = x[:kh] + x[kh:]
-        return x[:, :n] + x[:, n:]
+        total = x[:kh]
+        for i in range(1, x.shape[0] // kh):
+            total = total + x[i * kh : (i + 1) * kh]
+        return total[:, :n] + total[:, n:]
 
     def backward(misfit, alpha):
         weight[:, :n] = 2.0 * misfit
         weight[:, n:] = 2.0 * misfit
 
-        def pair(d, _):
+        def group(i, _):
+            first = i * GROUP
             y = weight[...]
-            f = spec[pair_rows(d), :]
+            f = spec[group_rows(first, GROUP), :]
             if alpha is not None:
-                f = f + alpha * moved[pair_rows(d), :]
-                spec[pair_rows(d), :] = f
-            half[:kh] = (f[:kh] * y).astype(BF16)
-            half[kh:] = (f[kh:] * y).astype(BF16)
+                f = f + alpha * moved[group_rows(first, GROUP), :]
+                spec[group_rows(first, GROUP), :] = f
+            for c in range(2 * GROUP):
+                half[c * kh : (c + 1) * kh] = (f[c * kh : (c + 1) * kh] * y).astype(BF16)
             b = dot(half[...], t_back[...]).astype(BF16)
-            for c in range(2):
+            for c in range(2 * GROUP):
                 turned[c, :kh] = b[c * kh : (c + 1) * kh, :n]
                 turned[c, kh:] = b[c * kh : (c + 1) * kh, n:]
                 g = dot(t_three[...], turned[c])
-                pr, pi = probes[d, c, 0], probes[d, c, 1]
+                d = first + c // 2
+                pr, pi = probes[d, c % 2, 0], probes[d, c % 2, 1]
                 patch[0] += pr * g[:n] + pi * g[n:]
                 patch[1] += pr * g[n:] - pi * g[:n]
             return 0
 
         clear(patch)
-        lax.fori_loop(0, n_ma, pair, 0, unroll=True)
+        lax.fori_loop(0, n_ma // GROUP, group, 0, unroll=True)
 
     def place(it):
         def part(p, _):
@@ -381,14 +393,16 @@
                     (tall.at[it, p, pl.ds(rim + tx + at, row_chunk)], from_z.at[it, 1, p, rows]),
                 )
             )
+        for p in range(2):
+            stack(tall[it, p, pl.ds(rim, tx)], terms_own, 0)
+            ext[it, p] = both(dot(terms_own[...], put_cols[:n]))
         sides = []
         for i, (p, at) in enumerate(chunks):
             rows = pl.ds(at, row_chunk)
             arrive(folds[i])
-            stack(tall[it, p, pl.ds(rim + at, row_chunk)], terms_put, 0)
-            stack(from_z[it, 1, p, rows], terms_put, n)
-            stack(from_z[it, 0, p, rows], terms_put, 2 * n)
-            ext[it, p, rows] = both(dot(terms_put[...], put_cols[...]))
+            stack(from_z[it, 1, p, rows], terms_put, 0)
+            stack(from_z[it, 0, p, rows], terms_put, n)
+            ext[it, p, rows] += both(dot(terms_put[...], put_cols[n:]))
             strip = ext.at[it, p, rows]
             sides.append(
                 exchange(
@@ -441,7 +455,9 @@
         stacked = []
         for i, (p, at) in enumerate(chunks):
             arrive(sides[i])
-            stacked.append(cut_and_lend(it + 1, p, at))
+            stacked.append(lend(it + 1, p, at, row_chunk))
+        for p in range(2):
+            keep(it + 1, p)
         for arrivals in stacked:
             arrive(arrivals)
         return square
@@ -481,8 +497,8 @@
     intensity = jnp.zeros((kh, n), F32)
 
     def add_spectra(d, total):
-        f = forward_pair(d)
-        spec[pair_rows(d), :] = f
+        f = forward(d, 1)
+        spec[group_rows(d, 1), :] = f
         return total + folded(f * f)
 
     other_part = 1 - mine_part
@@ -490,7 +506,7 @@
 
     def pass_on(d, h):
         ours = piece(d, mine_part, h)
-        passed[d, h] = send(ours, ours, gy_prev if h else gy_next)
+        passed[d, h] = send(ours, ours, gy_next if h < PIECES // 2 else gy_prev)
         handed[d, h] = send(ours, ours, partner)
 
     def hand_on(d, h):
@@ -499,42 +515,54 @@
         handed[d, h, 1] = send(theirs, theirs, partner)
 
     def complete(d):
-        for h in range(2):
+        for h in range(PIECES):
             handed[d, h].wait_recv()
             handed[d, h, 1].wait_recv()
 
     arrive(((down, above), (up, below)))
     set_columns(1)
     set_columns(2)
-    ring[1, 0].wait_recv()
-    ring[2, 0] = send(piece(1, mine_part, 0), piece(2, mine_part, 0), ma_next)
-    pass_on(1, 0)
-    ring[3, 1].wait_recv()
-    ring[2, 1] = send(piece(3, mine_part, 1), piece(2, mine_part, 1), ma_prev)
-    pass_on(3, 1)
+    for h in range(PIECES // 2):
+        g = PIECES - 1 - h
+        ring[1, h].wait_recv()
+        ring[2, h] = send(piece(1, mine_part, h), piece(2, mine_part, h), ma_next)
+        pass_on(1, h)
+        ring[3, g].wait_recv()
+        ring[2, g] = send(piece(3, mine_part, g), piece(2, mine_part, g), ma_prev)
+        pass_on(3, g)
     for p in range(2):
         arrive(first_beside[p])
-    stacked = [cut_and_lend(0, p, at) for p, at in chunks]
-    ring[1, 1].wait_recv()
-    pass_on(1, 1)
-    ring[3, 0].wait_recv()
-    pass_on(3, 0)
-    hand_on(1, 0)
-    hand_on(3, 1)
-    ring[2, 0].wait_recv()
-    pass_on(2, 0)
-    ring[2, 1].wait_recv()
-    pass_on(2, 1)
+    stacked = [lend(0, p, 0, tx) for p in range(2)]
+    for p in range(2):
+        keep(0, p)
+    for h in range(PIECES // 2):
+        g = PIECES - 1 - h
+        ring[1, g].wait_recv()
+        pass_on(1, g)
+        ring[3, h].wait_recv()
+        pass_on(3, h)
+    for h in range(PIECES // 2):
+        g = PIECES - 1 - h
+        hand_on(1, h)
+        hand_on(3, g)
+    for h in range(PIECES // 2):
+        g = PIECES - 1 - h
+        ring[2, h].wait_recv()
+        pass_on(2, h)
+        ring[2, g].wait_recv()
+        pass_on(2, g)
     for arrivals in stacked:
         arrive(arrivals)
     window(0)
-    hand_on(1, 1)
-    hand_on(3, 0)
+    for h in range(PIECES // 2):
+        g = PIECES - 1 - h
+        hand_on(1, g)
+        hand_on(3, h)
     intensity = add_spectra(0, intensity)
     complete(1)
     intensity = add_spectra(1, intensity)
-    hand_on(2, 0)
-    hand_on(2, 1)
+    for h in range(PIECES):
+        hand_on(2, h)
     complete(3)
     intensity = add_spectra(3, intensity)
     complete(2)
@@ -547,19 +575,21 @@
         window(it + 1)
         last = it + 1 == OUTER
 
-        def pair(d, change, last=last):
-            m = forward_pair(d)
+        def group(i, change, last=last):
+            rows = group_rows(i * GROUP, GROUP)
+            m = forward(i * GROUP, GROUP)
             if not last:
-                moved[pair_rows(d), :] = m
-            return change + folded(spec[pair_rows(d), :] * m)
-
-        change = 2.0 * lax.fori_loop(0, n_ma, pair, jnp.zeros((kh, n), F32), unroll=True)
+                moved[rows, :] = m
+            return change + folded(spec[rows, :] * m)
+
+        zeros = jnp.zeros((kh, n), F32)
+        change = 2.0 * lax.fori_loop(0, n_ma // GROUP, group, zeros, unroll=True)
         sums = step_size(it, square, squares(live * change))
         next(sums)
         if not last:
 
             def power(d, total):
-                m = moved[pair_rows(d), :]
+                m = moved[group_rows(d, 1), :]
                 return total + folded(m * m)
 
             moved_power = lax.fori_loop(0, n_ma, power, jnp.zeros((kh, n), F32))
@@ -596,11 +626,11 @@
             vmem((2 * n, 2 * n), BF16),
             vmem((2 * n, n), BF16),
             vmem((2, n, n), F32),
-            vmem((2, 2 * n, n), BF16),
-            vmem((n, 2 * n), BF16),
+            vmem((2 * GROUP, 2 * n, n), BF16),
+            vmem((GROUP * n, 2 * n), BF16),
             vmem((modes * kh, 2 * n), F32),
             vmem((modes * kh, 2 * n), F32),
-            vmem((2, n, n), BF16),
+            vmem((2 * GROUP, n, n), BF16),
             vmem((kh, 2 * n), F32),
             vmem((2, n, n), F32),
             vmem((OUTER, 2, height, n), F32),
@@ -609,10 +639,11 @@
             vmem((height, 2 * n), BF16),
             vmem((3 * n, width), BF16),
             vmem((3, 8, 128), F32),
-            vmem((2 * row_chunk, width), BF16),
+            vmem((2 * tx, width), BF16),
             vmem((2 * height, n), BF16),
             vmem((2 * n, n), BF16),
-            vmem((2 * row_chunk, 3 * n), BF16),
+            vmem((2 * row_chunk, 2 * n), BF16),
+            vmem((2 * tx, n), BF16),
             vmem((OUTER, 2, tx, width), F32),
             vmem((OUTER, 2, 2, tx, n), F32),
             vmem((OUTER, 2, 2, tx, rim), F32),
@@ -621,8 +652,8 @@
             vmem((OUTER, sizes[0], 1, 128), F32),
             pltpu.SemaphoreType.REGULAR((5,)),
             pltpu.SemaphoreType.DMA((6,)),
-            pltpu.SemaphoreType.DMA((112 + 56 * CHUNKS,)),
-            pltpu.SemaphoreType.DMA((112 + 56 * CHUNKS,)),
+            pltpu.SemaphoreType.DMA((88 + 12 * PIECES + 56 * CHUNKS,)),
+            pltpu.SemaphoreType.DMA((88 + 12 * PIECES + 56 * CHUNKS,)),
         ]
         anywhere = pl.BlockSpec(memory_space=pl.ANY)
         in_vmem = pl.BlockSpec(memory_space=pltpu.VMEM)

time: 103 us -> 102 us (level)
  Pallas kernels: 102 us -> 100 us
    pallas_call x1, Pallas kernels: 102 us -> 100 us  [shards(): pl.pallas_call(functools.partial(kernel, (*sizes, n, tx, ty)), out_shape=...]
where the time goes in v6:
time: 102 us
  Pallas kernels  100 us (98%)
    pallas_call x1, Pallas kernels, shards(): pl.pallas_call(functools.partial(kernel, (*sizes, n, tx, ty)), out_shape=...  100 us

profile of v6, /device:TPU:1, one launch (start us, length us, event | category | flops | bytes accessed | tf_op | source)
XLA Modules:
  0.0 101.5 jit_solution(5598803712662316275)
XLA Ops:
  0.7 0.0 copy-start
  0.7 100.1 %shard_map.64 = f32[2,128,256]{2,1,0:T(8,128)S(1)} custom-call(f32[2,128,256]{2,1,0:T(8,128)} %obj_hbm.1, f32[2,2,256,256]{3,2,1,0:T(8,128)} %probe_hbm.1, f32[1,1,2,256,256]{4,3,2,1,0:T(8,128)} %meas_hbm.1, s32[1,1,2,2]{3,2,1,0:T(2,128)} %pos_hbm.1, s32[1,1]{1,0:T(1,128)S(6)} %copy.7.count_hbm, bf16[2,256,256]{2,1,0:T(8,128)(2,1)} %constant.2.clone.w_hbm), custom_call_target="tpu_custom_call" | custom-call | tf_op jit(solution)/shard_map/pallas_call | solution.py:660
  100.8 0.0 copy-done
  100.8 0.7 add.3
Async XLA Ops:
  0.7 100.1 %copy-start = (f32[2,128,256]{2,1,0:T(8,128)S(1)}, f32[2,128,256]{2,1,0:T(8,128)}, u32[]{:S(2)}) copy-start(f32[2,128,256]{2,1,0:T(8,128)} %obj_hbm.1) | copy-start | bytes 786436
